TPU v7x, 512 devices: a whole 4x8x8 slice. The times are simulated.
512 devices in a mesh: dp: 32 (over z, x_lo, core), mp: 2 (over x_hi), pre: 8 (over y).
Axes of the slice: x: 4 (x_hi: 2, x_lo: 2; x = x_hi * 2 + x_lo), y: 8, z: 8, core: 2. Of those that a mesh axis runs over, the one named last changes fastest.
Arguments:
- activations: bfloat16 [49152, 1024], P('dp'), may hold values from -6 to 6
- grad_output: bfloat16 [49152, 4096], P('dp', ('mp', 'pre')), may hold values from -0.02734375 to 0.02734375
- left_old: float32 [1024, 1024], P(('mp', 'pre'), 'dp'), may hold values from -1 to 9, as said below
- right_old: float32 [4096, 4096], P(('mp', 'pre'), 'dp'), may hold values from -1 to 9, as said below
- probe_left: float32 [1024], replicated, may hold values from -6 to 6
- probe_right: float32 [4096], replicated, may hold values from -6 to 6
Outputs:
- left_new: float32 [1024, 1024], P(('mp', 'pre'), 'dp')
- right_new: float32 [4096, 4096], P(('mp', 'pre'), 'dp')
- update: float32 [1024, 4096], P('dp', ('mp', 'pre'))
Inputs may be any that keep to these rules, and one draw needn't show every extreme that they name: `left_old`: symmetric and positive definite. `right_old`: symmetric and positive definite.
All inputs are finite; a program needn't handle non-finite values.
Results may differ from a plain program's by a relative error of at most 0.0003.
Values sent between devices are 32-bit elements; how exact they have to be, the bound alone decides.
A program may use at most 64 MiB of HBM per device.

v0:
```python
import jax
import jax.numpy as jnp
from jax import lax
from jax.sharding import PartitionSpec as P

D = 1024
FF = 4096


beta_decay = 0.9
norm_floor = 1e-06


def split_up(shard, dim, devices):
    before, after = (shard.shape[:dim], shard.shape[dim + 1 :])
    return jnp.moveaxis(shard.reshape(*before, devices, -1, *after), dim, 0)


def sum_at_owner(shard, axis, dim):
    tiles = split_up(shard, dim, lax.axis_size(axis))
    arrived = lax.all_to_all(tiles, axis, split_axis=0, concat_axis=0, tiled=True)
    return arrived.sum(axis=0)


def sent_to_all(shard, axis):
    devices = lax.axis_size(axis)
    return lax.all_to_all(
        jnp.broadcast_to(shard[None], (devices, *shard.shape)), axis, 0, 0, tiled=True
    )


def laid_out(tiles, dim):
    tiles = jnp.moveaxis(tiles, 0, dim)
    dims = tiles.shape
    return tiles.reshape(*dims[:dim], dims[dim] * dims[dim + 1], *dims[dim + 2 :])


def gathered_copies(shard, axis, dim):
    tiles = sent_to_all(shard, axis)
    return laid_out(tiles, dim)


def picked(shard, axis, root):
    return lax.dynamic_index_in_dim(lax.all_gather(shard, axis), root, 0, keepdims=False)


def taken_together(shard, axis):
    return sent_to_all(shard, axis).sum(axis=0)


def in_one(arrays, axis):
    line, at, gathered = (jnp.concatenate([a.reshape(-1) for a in arrays]), 0, [])
    total = taken_together(line, axis)
    for a in arrays:
        gathered.append(total[at : at + a.size].reshape(a.shape))
        at += a.size
    return tuple(gathered)


def gather_together(arrays, axis, dims):
    line = jnp.concatenate([a.reshape(-1) for a in arrays])
    lines, at, gathered = (lax.all_gather(line, axis), 0, [])
    for a, dim in zip(arrays, dims):
        tiles = lines[:, at : at + a.size].reshape(-1, *a.shape)
        gathered.append(laid_out(tiles, dim))
        at += a.size
    return tuple(gathered)


def length_of(vector):
    return jnp.sqrt(jnp.sum(vector * vector) + norm_floor)


def shards(activations, grad_output, left_old, right_old, probe_left, probe_right):
    highest = lax.Precision.HIGHEST
    data_count = lax.axis_size("dp")
    model_count = lax.axis_size(("mp", "pre"))
    data_index = lax.axis_index("dp")
    model_index = lax.axis_index(("mp", "pre"))
    model_width = activations.shape[1]
    block_cols = grad_output.shape[1]
    own_count = model_width // data_count
    left_count = model_width // model_count
    group_ratio = data_count // model_count
    panel_width = block_cols // group_ratio
    panel_offset = data_index % group_ratio * panel_width
    panel_owner = data_index // group_ratio
    contract_first = (((0,), (0,)), ((), ()))
    grad_rows = sum_at_owner(
        lax.dot_general(
            activations, grad_output, contract_first, preferred_element_type=jnp.float32
        ),
        "dp",
        0,
    )
    grad_block = gathered_copies(grad_rows, "dp", 0)
    grad_panel = picked(
        lax.dynamic_slice_in_dim(grad_block, panel_offset, panel_width, 1),
        ("mp", "pre"),
        panel_owner,
    )
    left_new = beta_decay * left_old + sum_at_owner(
        lax.dot_general(
            grad_block,
            grad_rows,
            (((1,), (1,)), ((), ())),
            precision=highest,
            preferred_element_type=jnp.float32,
        )
        / FF,
        ("mp", "pre"),
        0,
    )
    right_gram = lax.dot_general(
        grad_block,
        grad_panel,
        contract_first,
        precision=highest,
        preferred_element_type=jnp.float32,
    )
    right_new = beta_decay * right_old + right_gram / D

    def power_sweep(vector_left, vector_right):
        slice_left = lax.dynamic_slice_in_dim(vector_left, data_index * own_count, own_count, 0)
        slice_right = lax.dynamic_slice_in_dim(
            vector_right, data_index * panel_width, panel_width, 0
        )
        part_left = jnp.dot(
            left_new, slice_left, precision=highest, preferred_element_type=jnp.float32
        )
        part_right = jnp.dot(
            right_new, slice_right, precision=highest, preferred_element_type=jnp.float32
        )
        summed_left, summed_right = in_one((part_left, part_right), "dp")
        joined = gather_together((summed_left, summed_right), ("mp", "pre"), (0, 0))
        return joined

    image_left, image_right = power_sweep(probe_left, probe_right)
    unit_left = image_left / length_of(image_left)
    unit_right = image_right / length_of(image_right)
    image_left, image_right = power_sweep(unit_left, unit_right)
    top_left = length_of(image_left)
    top_right = length_of(image_right)
    left_rows = gathered_copies(left_new, "dp", 1)
    grad_part = lax.dynamic_slice_in_dim(grad_panel, model_index * left_count, left_count, 0)
    left_terms = lax.dot_general(
        left_rows, grad_part, contract_first, precision=highest, preferred_element_type=jnp.float32
    )
    product = lax.psum(left_terms, ("mp", "pre"))
    step_panel = (5.0 * grad_panel - product / top_left) * 0.25
    row_ids = lax.broadcasted_iota(jnp.int32, (panel_width, block_cols), 0) + panel_offset
    col_ids = lax.broadcasted_iota(jnp.int32, (panel_width, block_cols), 1)
    identity_part = jnp.where((row_ids == col_ids) & (panel_owner == model_index), 1.0, 0.0).astype(
        jnp.float32
    )
    right_mix = (5.0 * identity_part - right_new.T / top_right) * 0.25
    update = sum_at_owner(
        jnp.dot(step_panel, right_mix, precision=highest, preferred_element_type=jnp.float32),
        "dp",
        0,
    ) * (top_left * top_right) ** (-0.25)
    return (left_new, right_new, update)


def solution(mesh):
    in_specs = (
        P("dp", None),
        P("dp", ("mp", "pre")),
        P(("mp", "pre"), "dp"),
        P(("mp", "pre"), "dp"),
        P(),
        P(),
    )
    out_specs = (P(("mp", "pre"), "dp"), P(("mp", "pre"), "dp"), P("dp", ("mp", "pre")))
    return jax.shard_map(shards, mesh=mesh, in_specs=in_specs, out_specs=out_specs, check_vma=False)
```

profile of v0, /device:TPU:1, one launch (start us, length us, event | category | flops | bytes accessed | tf_op | source)
XLA Modules:
  0.0 460.6 jit_solution(10846822143533983472)
XLA Ops:
  7.2 0.0 copy-start
  7.2 1.9 copy-done
  9.1 3.2 fusion.48
  12.2 12.9 %all-to-all-start = ((f32[32,32,256]{2,1,0:T(8,128)}), f32[32,32,256]{2,1,0:T(8,128)}, u32[]{:S(2)}, u32[]{:S(2)}) async-start(f32[32,32,256]{2,1,0:T(8,128)} %bitcast.68), calls=%async_computation | async-start | bytes 2097152 | tf_op jit(solution)/shard_map/all_to_all | solution.py:21
  25.2 28.1 %all-to-all-done = f32[32,32,256]{2,1,0:T(8,128)} async-done(((f32[32,32,256]{2,1,0:T(8,128)}), f32[32,32,256]{2,1,0:T(8,128)}, u32[]{:S(2)}, u32[]{:S(2)}) %all-to-all-start) | async-done | bytes 1048608 | tf_op jit(solution)/shard_map/all_to_all | solution.py:21
  53.3 1.3 reduce_sum.81
  54.6 1.1 broadcast_in_dim.14
  55.7 5.0 %all-to-all-start.1 = ((f32[32,32,256]{2,1,0:T(8,128)}), f32[32,32,256]{2,1,0:T(8,128)}, u32[]{:S(2)}, u32[]{:S(2)}) async-start(f32[32,32,256]{2,1,0:T(8,128)} %broadcast_in_dim.14), calls=%async_computation.1 | async-start | bytes 2097152 | tf_op jit(solution)/shard_map/all_to_all | solution.py:27
  60.7 0.0 all-gather.5.cloned.1.call-start
  60.8 28.0 %all-to-all-done.1 = f32[32,32,256]{2,1,0:T(8,128)} async-done(((f32[32,32,256]{2,1,0:T(8,128)}), f32[32,32,256]{2,1,0:T(8,128)}, u32[]{:S(2)}, u32[]{:S(2)}) %all-to-all-start.1) | async-done | bytes 1048608 | tf_op jit(solution)/shard_map/all_to_all | solution.py:27
  88.8 1.9 constant_dynamic-slice_fusion
  90.6 0.0 all-gather.5.cloned.1.call-update
  90.7 2.3 convolution_multiply_fusion
  92.9 0.1 reshape.46
  93.0 0.8 copy.19
  93.8 1.1 reshape.70
  95.0 18.3 %all_to_all.37 = f32[16,1,2048]{2,1,0:T(1,128)S(1)} all-to-all(f32[16,1,2048]{2,1,0:T(1,128)S(1)} %reshape.70), channel_id=1, replica_groups=mesh['dp'=32,'mp'=2,'pre'=8] {'mp','pre'}, dimensions={0} | all-to-all | bytes 262144 | tf_op jit(solution)/shard_map/all_to_all | solution.py:21
  113.3 0.5 broadcast.22
  113.8 0.9 reduce.6
  114.7 0.1 reshape.71
  114.9 0.8 broadcast_bitcast_fusion
  115.8 2.1 reshape.72
  117.8 7.5 %all-to-all-start.3 = ((f32[32,1,2048]{2,1,0:T(1,128)}), f32[32,1,2048]{2,1,0:T(1,128)}, u32[]{:S(2)}, u32[]{:S(2)}) async-start(f32[32,1,2048]{2,1,0:T(1,128)} %reshape.72), calls=%async_computation.3 | async-start | bytes 524288 | tf_op jit(solution)/shard_map/all_to_all | solution.py:27
  125.4 1.3 dynamic-slice.2
  127.4 0.9 convolution_bitcast_fusion.1
  128.2 8.7 %all-to-all-done.3 = f32[32,1,2048]{2,1,0:T(1,128)} async-done(((f32[32,1,2048]{2,1,0:T(1,128)}), f32[32,1,2048]{2,1,0:T(1,128)}, u32[]{:S(2)}, u32[]{:S(2)}) %all-to-all-start.3) | async-done | bytes 262176 | tf_op jit(solution)/shard_map/all_to_all | solution.py:27
  136.9 2.2 reduce.7
  139.2 1.0 reshape.73
  140.2 87.2 %all-gather.5.cloned.1.call-done = f32[16384,128]{1,0:T(8,128)} async-done(((f32[1024,128]{1,0:T(8,128)}), f32[16384,128]{1,0:T(8,128)}) %all-gather.5.cloned.1.call-update) | async-done | bytes 8388624 | tf_op jit(solution)/shard_map/all_gather | solution.py:44
  227.4 3.2 fusion
  230.6 0.9 fusion.37
  231.6 0.1 pad_maximum_fusion
  231.7 0.7 broadcast_in_dim.16
  232.3 8.9 %all-to-all-start.4 = ((f32[32,1,320]{2,1,0:T(1,128)}), f32[32,1,320]{2,1,0:T(1,128)S(1)}, u32[]{:S(2)}, u32[]{:S(2)}) async-start(f32[32,1,320]{2,1,0:T(1,128)} %broadcast_in_dim.16), calls=%async_computation.4 | async-start | bytes 98304 | tf_op jit(solution)/shard_map/all_to_all | solution.py:27
  241.3 0.0 all-reduce.4.cloned.1.call-start
  241.3 2.5 fusion.26
  243.8 0.0 all-reduce.4.cloned.1.call-update
  243.8 5.6 %all-to-all-done.4 = f32[32,1,320]{2,1,0:T(1,128)S(1)} async-done(((f32[32,1,320]{2,1,0:T(1,128)}), f32[32,1,320]{2,1,0:T(1,128)S(1)}, u32[]{:S(2)}, u32[]{:S(2)}) %all-to-all-start.4) | async-done | bytes 40992 | tf_op jit(solution)/shard_map/all_to_all | solution.py:27
  249.4 0.1 reduce_sum.83
  249.5 0.3 dynamic-update-slice
  249.8 61.9 %all-reduce = f32[5120]{0:T(1024)S(1)} all-reduce(f32[5120]{0:T(1024)S(1)} %dynamic-update-slice), channel_id=3, replica_groups=mesh['dp'=32,'mp'=2,'pre'=8] {'mp','pre'}, use_global_device_ids=true, to_apply=%add | all-reduce | flops 5120 | bytes 40960
  311.7 0.1 reshape.50
  311.7 0.7 multiply_reduce_fusion
  312.4 0.6 multiply_reduce_fusion.1
  313.7 0.1 divide_bitcast_fusion
  313.8 0.2 fusion.34
  314.8 0.1 div.62
  314.9 0.2 convolution_bitcast_fusion
  315.1 0.1 pad_maximum_fusion.1
  315.1 0.7 broadcast_in_dim.17
  315.8 16.6 %all-to-all-start.5 = ((f32[32,1,320]{2,1,0:T(1,128)}), f32[32,1,320]{2,1,0:T(1,128)S(1)}, u32[]{:S(2)}, u32[]{:S(2)}) async-start(f32[32,1,320]{2,1,0:T(1,128)} %broadcast_in_dim.17), calls=%async_computation.5 | async-start | bytes 98304 | tf_op jit(solution)/shard_map/all_to_all | solution.py:27
  332.5 8.3 %all-to-all-done.5 = f32[32,1,320]{2,1,0:T(1,128)S(1)} async-done(((f32[32,1,320]{2,1,0:T(1,128)}), f32[32,1,320]{2,1,0:T(1,128)S(1)}, u32[]{:S(2)}, u32[]{:S(2)}) %all-to-all-start.5) | async-done | bytes 40992 | tf_op jit(solution)/shard_map/all_to_all | solution.py:27
  340.7 0.1 reduce_sum.86
  340.8 0.3 dynamic-update-slice.1
  341.1 61.7 %all-reduce.1 = f32[5120]{0:T(1024)S(1)} all-reduce(f32[5120]{0:T(1024)S(1)} %dynamic-update-slice.1), channel_id=4, replica_groups=mesh['dp'=32,'mp'=2,'pre'=8] {'mp','pre'}, use_global_device_ids=true, to_apply=%add.1 | all-reduce | flops 5120 | bytes 40960
  402.8 0.1 reshape.51
  402.9 0.6 fusion.30
  404.2 0.7 fusion.29
  405.5 0.0 all-reduce.4.cloned.1.call-done
  405.6 3.3 fusion.4
  408.8 14.9 %all-to-all-start.6 = ((f32[32,32,256]{2,1,0:T(8,128)}), f32[32,32,256]{2,1,0:T(8,128)}, u32[]{:S(2)}, u32[]{:S(2)}) async-start(f32[32,32,256]{2,1,0:T(8,128)} %bitcast.67), calls=%async_computation.6 | async-start | bytes 2097152 | tf_op jit(solution)/shard_map/all_to_all | solution.py:21
  423.8 28.0 %all-to-all-done.6 = f32[32,32,256]{2,1,0:T(8,128)} async-done(((f32[32,32,256]{2,1,0:T(8,128)}), f32[32,32,256]{2,1,0:T(8,128)}, u32[]{:S(2)}, u32[]{:S(2)}) %all-to-all-start.6) | async-done | bytes 1048608 | tf_op jit(solution)/shard_map/all_to_all | solution.py:21
  451.8 1.3 reduce_sum.89
  453.1 0.6 broadcast_multiply_fusion
  (13 shorter events, 0.1 us)
Async XLA Ops:
  7.2 1.9 copy-start
  7.2 107.7 %copy-start.3 = (f32[64,32]{0,1:T(8,128)S(1)}, f32[64,32]{0,1:T(8,128)}, u32[]{:S(2)}) copy-start(f32[64,32]{0,1:T(8,128)} %param.8) | copy-start | bytes 24580
  12.2 41.1 %all-to-all-start = ((f32[32,32,256]{2,1,0:T(8,128)}), f32[32,32,256]{2,1,0:T(8,128)}, u32[]{:S(2)}, u32[]{:S(2)}) async-start(f32[32,32,256]{2,1,0:T(8,128)} %bitcast.68), calls=%async_computation | async-start | bytes 2097152 | tf_op jit(solution)/shard_map/all_to_all | solution.py:21
  55.7 33.0 %all-to-all-start.1 = ((f32[32,32,256]{2,1,0:T(8,128)}), f32[32,32,256]{2,1,0:T(8,128)}, u32[]{:S(2)}, u32[]{:S(2)}) async-start(f32[32,32,256]{2,1,0:T(8,128)} %broadcast_in_dim.14), calls=%async_computation.1 | async-start | bytes 2097152 | tf_op jit(solution)/shard_map/all_to_all | solution.py:27
  60.7 166.7 %all-gather.5.cloned.1.call-start = ((), (), s32[]{:S(2)}) async-start(), calls=%async_computation.8 | async-start | bytes 8912896 | tf_op jit(solution)/shard_map/all_gather | solution.py:44
  114.9 338.8 %copy-start.2 = (f32[64,32]{0,1:T(8,128)}, f32[64,32]{0,1:T(8,128)S(1)}, u32[]{:S(2)}) copy-start(f32[64,32]{0,1:T(8,128)S(1)} %multiply_add_fusion) | copy-start | bytes 24580
  117.8 19.1 %all-to-all-start.3 = ((f32[32,1,2048]{2,1,0:T(1,128)}), f32[32,1,2048]{2,1,0:T(1,128)}, u32[]{:S(2)}, u32[]{:S(2)}) async-start(f32[32,1,2048]{2,1,0:T(1,128)} %reshape.72), calls=%async_computation.3 | async-start | bytes 524288 | tf_op jit(solution)/shard_map/all_to_all | solution.py:27
  230.6 223.1 %copy-start.1 = (f32[256,128]{1,0:T(8,128)}, f32[256,128]{1,0:T(8,128)S(1)}, u32[]{:S(2)}) copy-start(f32[256,128]{1,0:T(8,128)S(1)} %fusion) | copy-start | bytes 393220
  232.3 17.1 %all-to-all-start.4 = ((f32[32,1,320]{2,1,0:T(1,128)}), f32[32,1,320]{2,1,0:T(1,128)S(1)}, u32[]{:S(2)}, u32[]{:S(2)}) async-start(f32[32,1,320]{2,1,0:T(1,128)} %broadcast_in_dim.16), calls=%async_computation.4 | async-start | bytes 98304 | tf_op jit(solution)/shard_map/all_to_all | solution.py:27
  241.3 164.3 %all-reduce.4.cloned.1.call-start = ((), (), s32[]{:S(2)}) async-start(), calls=%async_computation.7 | async-start | bytes 1048576 | tf_op jit(solution)/shard_map/psum | solution.py:149
  315.8 24.9 %all-to-all-start.5 = ((f32[32,1,320]{2,1,0:T(1,128)}), f32[32,1,320]{2,1,0:T(1,128)S(1)}, u32[]{:S(2)}, u32[]{:S(2)}) async-start(f32[32,1,320]{2,1,0:T(1,128)} %broadcast_in_dim.17), calls=%async_computation.5 | async-start | bytes 98304 | tf_op jit(solution)/shard_map/all_to_all | solution.py:27
  408.8 43.0 %all-to-all-start.6 = ((f32[32,32,256]{2,1,0:T(8,128)}), f32[32,32,256]{2,1,0:T(8,128)}, u32[]{:S(2)}, u32[]{:S(2)}) async-start(f32[32,32,256]{2,1,0:T(8,128)} %bitcast.67), calls=%async_computation.6 | async-start | bytes 2097152 | tf_op jit(solution)/shard_map/all_to_all | solution.py:21
Sparse Core Ops, SparseCore 0:
  90.8 136.5 all-gather.4
  245.0 149.0 all-reduce.3
where the time goes:
time: 462 us; the launch traced here: 461 us
  waiting for transfers between devices  194 us (42%)
  blocking collectives  142 us (31%)
  starting transfers between devices  66 us (14%)
  between operations  17.8 us (4%)
  matrix products  16.7 us (4%)
  local copies, waits for them, and re-layouts  14.8 us (3%)
  other arithmetic  9.4 us (2%)
    unnamed x2, blocking collectives  124 us
    all_gather x1, waiting for transfers between devices, picked(): lax.all_gather(shard, axis)  87.2 us
    all_to_all x2, waiting for transfers between devices, sum_at_owner(): lax.all_to_all(tiles, axis, split_axis=0, concat_axis=0, tiled=True)  56.1 us
    all_to_all x4, waiting for transfers between devices, sent_to_all(): lax.all_to_all(jnp.broadcast_to(shard[None], (devices, *shard.shape)), ax...  50.6 us
    all_to_all x4, starting transfers between devices, sent_to_all(): lax.all_to_all(jnp.broadcast_to(shard[None], (devices, *shard.shape)), ax...  38.1 us
    all_to_all x2, starting transfers between devices, sum_at_owner(): lax.all_to_all(tiles, axis, split_axis=0, concat_axis=0, tiled=True)  27.8 us
    all_to_all x1, blocking collectives, sum_at_owner(): lax.all_to_all(tiles, axis, split_axis=0, concat_axis=0, tiled=True)  18.3 us
  transfers between devices with their start and end apart: 8, of which 7 were waited for; matrix products, arithmetic and copies ran while one was open for 5% of the time, Pallas kernels for 0%

commit v1 on v0

v1 whole, which is shorter than its diff:
```python
import functools

import jax
import jax.numpy as jnp
from jax import lax
from jax.experimental import pallas as pl
from jax.experimental.pallas import tpu as pltpu
from jax.sharding import PartitionSpec as P

MESH = pl.DeviceIdType.MESH
F32 = jnp.float32
BF16 = jnp.bfloat16

DECAY = 0.9
FLOOR = 1e-06
SLAB = 64
HALF = 128
COPIES = 176

NN = (((1,), (0,)), ((), ()))
NT = (((1,), (1,)), ((), ()))
TN = (((0,), (0,)), ((), ()))


def far_first(n):
    return sorted(range(1, n), key=lambda o: -min(o, n - o))


def near_first(n):
    return sorted(range(1, n), key=lambda o: min(o, n - o))


def halves(v):
    high = v.astype(BF16)
    return high, (v - high.astype(F32)).astype(BF16)


def dot3(a, b, dims):
    (ah, al), (bh, bl) = a, b
    dot = functools.partial(lax.dot_general, dimension_numbers=dims, preferred_element_type=F32)
    return dot(ah, bh) + (dot(ah, bl) + dot(al, bh))


class Net:
    def __init__(self, send_sem, recv_sem):
        self.send_sem, self.recv_sem, self.used, self.sent = send_sem, recv_sem, 0, []

    def slot(self):
        self.used += 1
        assert self.used <= COPIES
        return self.used - 1

    def copy(self, i, src, dst, device):
        return pltpu.make_async_remote_copy(
            src_ref=src,
            dst_ref=dst,
            send_sem=self.send_sem.at[i],
            recv_sem=self.recv_sem.at[i],
            device_id=device,
            device_id_type=MESH,
        )

    def send(self, i, src, dst, device):
        copy = self.copy(i, src, dst, device)
        copy.start()
        self.sent.append(copy)

    def arrive(self, i, dst, device):
        self.copy(i, dst, dst, device).wait_recv()

    def finish(self):
        for copy in self.sent:
            copy.wait_send()


def kernel(
    nz,
    ny,
    ff,
    act,
    dy,
    left_old,
    right_old,
    p_left,
    p_right,
    left_out,
    right_out,
    update_out,
    part,
    rc,
    xs,
    rx,
    zs,
    rz,
    grad,
    part2,
    rc2,
    xs2,
    rx2,
    zs2,
    rz2,
    prod,
    gown,
    panel,
    rtile,
    lpart,
    lr,
    lsum,
    lx,
    lrow,
    square,
    square2,
    abuf,
    arecv,
    azrecv,
    bbuf,
    brecv,
    byrecv,
    cbuf,
    crecv,
    czrecv,
    send_sem,
    recv_sem,
):
    d_model = nz * 2 * SLAB
    rows_l = d_model // 128
    dp, mp, pre = lax.axis_index("dp"), lax.axis_index("mp"), lax.axis_index("pre")
    z, xl, c = dp // 4, (dp // 2) % 2, dp % 2
    a = mp * ny + pre
    b = z * 2 + xl
    on_diagonal = a == b

    core_peer = (dp + 1 - 2 * c, mp, pre)
    x_peer = (dp + 2 - 4 * xl, mp, pre)
    hi_peer = (dp, 1 - mp, pre)
    flip_peer = (a * 2 + c, b // ny, b % ny)

    def z_at(o):
        return (z + o) % nz

    def z_peer(o):
        return (z_at(o) * 4 + xl * 2 + c, mp, pre)

    def y_at(o):
        return (pre + o) % ny

    def y_peer(o):
        return (dp, mp, y_at(o))

    net = Net(send_sem, recv_sem)

    barrier = pltpu.get_barrier_semaphore()

    def greet(device):
        pl.semaphore_signal(barrier, inc=1, device_id=device, device_id_type=MESH)

    greet(core_peer)
    greet(x_peer)
    greet(hi_peer)
    for o in range(1, nz):
        greet(z_peer(o))
    for o in range(1, ny):
        greet(y_peer(o))

    @pl.when(jnp.logical_not(on_diagonal))
    def _():
        greet(flip_peer)

    def slab_rows(z_, xl_):
        return pl.ds(pl.multiple_of((z_ * 2 + xl_) * SLAB, SLAB), SLAB)

    def pair_rows(z_):
        return pl.ds(pl.multiple_of(z_ * 2 * SLAB, 2 * SLAB), 2 * SLAB)

    def half_cols(c_):
        return pl.ds(pl.multiple_of(c_ * HALF, HALF), HALF)

    mine, other = half_cols(c), half_cols(1 - c)
    z_order = far_first(nz) + [0]

    class Scatter:
        def __init__(self, part, rc, xs, rx, zs, rz):
            self.part, self.rc, self.xs, self.rx, self.zs, self.rz = part, rc, xs, rx, zs, rz
            self.ic = [net.slot() for _ in range(nz)]
            self.ix = [net.slot() for _ in range(nz)]
            self.iz = [net.slot() for _ in range(nz)]

        def block(self, o, value):
            rows = pair_rows(z_at(o))
            self.part[rows, :] = value
            net.send(self.ic[o], self.part.at[rows, other], self.rc.at[rows, :], core_peer)

        def over_x(self, o):
            rows = pair_rows(z_at(o))
            net.arrive(self.ic[o], self.rc.at[rows, :], core_peer)
            theirs = slab_rows(z_at(o), 1 - xl)
            self.xs[o] = self.part[theirs, mine] + self.rc[theirs, :]
            net.send(self.ix[o], self.xs.at[o], self.rx.at[o], x_peer)

        def over_z(self, o):
            net.arrive(self.ix[o], self.rx.at[o], x_peer)
            ours = slab_rows(z_at(o), xl)
            self.zs[o] = self.part[ours, mine] + self.rc[ours, :] + self.rx[o]
            if o:
                net.send(self.iz[o], self.zs.at[o], self.rz.at[o], z_peer(o))

        def total(self):
            value = self.zs[0]
            for o in near_first(nz):
                net.arrive(self.iz[o], self.rz.at[o], z_peer(o))
                value = value + self.rz[o]
            return value

    class Gather:
        def __init__(self, full):
            self.full = full
            self.ic = [net.slot() for _ in range(nz)]
            self.ix = [net.slot() for _ in range(nz)]
            self.iz = [net.slot() for _ in range(nz)]

        def over_z(self, value):
            rows = slab_rows(z, xl)
            self.full[rows, mine] = value
            chunk = self.full.at[rows, mine]
            for o in far_first(nz):
                net.send(self.iz[o], chunk, chunk, z_peer(o))
            net.send(self.ix[0], chunk, chunk, x_peer)

        def over_x(self, o):
            chunk = self.full.at[slab_rows(z_at(nz - o), xl), mine]
            net.arrive(self.iz[o], chunk, z_peer(nz - o))
            net.send(self.ix[o], chunk, chunk, x_peer)

        def over_core(self, o):
            z_ = z_at(nz - o)
            net.arrive(self.ix[o], self.full.at[slab_rows(z_, 1 - xl), mine], x_peer)
            pair = self.full.at[pair_rows(z_), mine]
            net.send(self.ic[o], pair, pair, core_peer)

        def landed(self, o):
            net.arrive(self.ic[o], self.full.at[pair_rows(z_at(nz - o)), other], core_peer)

    first = Scatter(part, rc, xs, rx, zs, rz)
    gather = Gather(grad)

    def grad_block(o):
        cols = pl.ds(pl.multiple_of(z_at(o) * 128, 128), 128)
        return lax.dot_general(act[:, cols], dy[...], TN, preferred_element_type=F32)

    first_value = grad_block(z_order[0])
    count = 3 + (nz - 1) + (ny - 1)
    pl.semaphore_wait(barrier, count + jnp.where(on_diagonal, 0, 1))
    first.block(z_order[0], first_value)
    for o in z_order[1:]:
        first.block(o, grad_block(o))
    for o in z_order:
        first.over_x(o)
    for o in z_order:
        first.over_z(o)
    gown[...] = first.total()

    i_flip = net.slot()
    iy = [net.slot() for _ in range(ny)]
    ih = [net.slot() for _ in range(ny)]

    def a_rows(mp_, y_):
        return pl.ds(pl.multiple_of((mp_ * ny + y_) * SLAB, SLAB), SLAB)

    own_rows = a_rows(mp, pre)
    flip_rows = pl.ds(pl.multiple_of(b * SLAB, SLAB), SLAB)

    @pl.when(jnp.logical_not(on_diagonal))
    def _():
        net.copy(i_flip, gown, panel.at[flip_rows, :], flip_peer).start()

    @pl.when(on_diagonal)
    def _():
        panel[own_rows, :] = gown[...]

    gather.over_z(gown[...])
    for o in near_first(nz)[: nz // 2]:
        gather.over_x(o)

    @pl.when(jnp.logical_not(on_diagonal))
    def _():
        net.copy(i_flip, gown, panel.at[own_rows, :], flip_peer).wait_recv()

    own_panel = panel.at[own_rows, :]
    for o in far_first(ny):
        net.send(iy[o], own_panel, own_panel, y_peer(o))
    net.send(ih[0], own_panel, own_panel, hi_peer)
    for o in near_first(nz)[nz // 2 :]:
        gather.over_x(o)
    for o in [0] + near_first(nz):
        gather.over_core(o)

    def panel_over_hi(o):
        chunk = panel.at[a_rows(mp, y_at(ny - o)), :]
        net.arrive(iy[o], chunk, y_peer(ny - o))
        net.send(ih[o], chunk, chunk, hi_peer)

    for o in near_first(ny)[: ny // 2]:
        panel_over_hi(o)
    for o in [0] + near_first(nz):
        gather.landed(o)

    il = [net.slot() for _ in range(ny)]
    ilx = net.slot()
    ilg = [net.slot() for _ in range(ny)]
    grad_high, grad_low = halves(grad[...])
    own_grad = grad[pl.ds(pl.multiple_of(dp * 32, 32), 32), :]
    lpart[...] = dot3(halves(own_grad), (grad_high, grad_low), NT) * (1.0 / ff)
    square[...] = jnp.zeros_like(square)
    square[pl.ds(pl.multiple_of((a % 2) * SLAB, SLAB), SLAB), pl.ds(0, 32)] = (
        left_old[...] * DECAY
    )
    old_lanes = pl.ds(pl.multiple_of((a // 2) * 128, 128), 128)
    square2[...] = square[...].T
    lpart[:, old_lanes] += square2[pl.ds(0, 32), :]

    def l_lanes(y_):
        return pl.ds(pl.multiple_of(y_ * 128, 128), 128)

    for o in far_first(ny):
        net.send(il[o], lpart.at[:, l_lanes(y_at(o))], lr.at[o], y_peer(o))
    for o in near_first(ny)[ny // 2 :]:
        panel_over_hi(o)
    total = lpart[:, l_lanes(pre)]
    for o in near_first(ny):
        net.arrive(il[o], lr.at[o], y_peer(o))
        total = total + lr[o]
    lsum[...] = total
    net.send(ilx, lsum, lx, hi_peer)
    for o in [0] + near_first(ny):
        net.arrive(ih[o], panel.at[a_rows(1 - mp, y_at(ny - o)), :], hi_peer)

    panel_high, panel_low = halves(panel[...])
    panel_t = halves(panel[...].T)
    gram = dot3(panel_t, (grad_high, grad_low), NN)
    rtile[...] = right_old[...].T * DECAY + gram * (1.0 / d_model)

    net.arrive(ilx, lx, hi_peer)
    lrow[:, l_lanes(pre)] = lsum[...] + lx[...]
    own_lanes = lrow.at[:, l_lanes(pre)]
    for o in far_first(ny):
        net.send(ilg[o], own_lanes, own_lanes, y_peer(o))

    second = Scatter(part2, rc2, xs2, rx2, zs2, rz2)
    gather2 = Gather(prod)
    rt_split = halves(rtile[...])
    part_panel = (panel_high, panel_low)

    def prod_block(o):
        rows = pair_rows(z_at(o))
        return dot3(halves(panel[rows, :]), rt_split, NN)

    for o in z_order:
        second.block(o, prod_block(o))
    for o in z_order:
        second.over_x(o)

    for o in near_first(ny):
        net.arrive(ilg[o], lrow.at[:, l_lanes(y_at(ny - o))], y_peer(ny - o))
    square[...] = jnp.zeros_like(square)
    square[pl.ds(0, rows_l), :] = p_left[...]
    lane = lax.broadcasted_iota(jnp.int32, (128, 128), 1)
    column = jnp.sum(jnp.where(lane == dp // 4, square[...].T, 0.0), axis=1, keepdims=True)
    square2[...] = jnp.broadcast_to(column, (128, 128))
    p_col = square2[pl.ds(pl.multiple_of((dp % 4) * 32, 32), 32), pl.ds(0, 1)]
    first_left = jnp.sum(lrow[...] * p_col, axis=0, keepdims=True)
    p_row = jnp.broadcast_to(p_right[pl.ds(dp, 1), :], (8, 128))
    first_right = dot3(halves(p_row), rt_split, NN)
    abuf[0] = jnp.zeros_like(abuf[0])
    for j in range(rows_l):
        abuf[0, pl.ds(j, 1), :] = first_left[:, j * 128 : (j + 1) * 128]
    abuf[0, pl.ds(8, 1), :] = first_right[0:1, :128]
    abuf[0, pl.ds(9, 1), :] = first_right[0:1, 128:]

    class Sum:
        def __init__(self, buf, recv, zrecv):
            self.buf, self.recv, self.zrecv = buf, recv, zrecv
            self.ic, self.ix = net.slot(), net.slot()
            self.iz = [net.slot() for _ in range(nz)]

        def over_core(self):
            net.send(self.ic, self.buf.at[0], self.recv.at[0], core_peer)

        def over_x(self):
            net.arrive(self.ic, self.recv.at[0], core_peer)
            self.buf[1] = self.buf[0] + self.recv[0]
            net.send(self.ix, self.buf.at[1], self.recv.at[1], x_peer)

        def over_z(self):
            net.arrive(self.ix, self.recv.at[1], x_peer)
            self.buf[2] = self.buf[1] + self.recv[1]
            for o in far_first(nz):
                net.send(self.iz[o], self.buf.at[2], self.zrecv.at[o], z_peer(o))

        def total(self):
            value = self.buf[2]
            for o in near_first(nz):
                net.arrive(self.iz[o], self.zrecv.at[o], z_peer(o))
                value = value + self.zrecv[o]
            return value

    asum = Sum(abuf, arecv, azrecv)
    csum = Sum(cbuf, crecv, czrecv)
    asum.over_core()
    for o in z_order[: nz // 2]:
        second.over_z(o)
    asum.over_x()
    for o in z_order[nz // 2 :]:
        second.over_z(o)
    asum.over_z()
    gather2.over_z(second.total())

    images = asum.total()
    f_left = images[0:rows_l, :]
    norm_left = jnp.sqrt(
        jnp.sum(jnp.sum(f_left * f_left, axis=1, keepdims=True), axis=0, keepdims=True) + FLOOR
    )
    unit_left = f_left / norm_left
    second_left = jnp.zeros((32, 1), F32)
    for j in range(rows_l):
        second_left = second_left + jnp.sum(
            lrow[:, j * 128 : (j + 1) * 128] * unit_left[j : j + 1, :], axis=1, keepdims=True
        )
    left_square = jnp.sum(second_left * second_left, axis=0, keepdims=True)
    f_low, f_high = images[8:9, :], images[9:10, :]
    right_square = jnp.sum(f_low * f_low + f_high * f_high, axis=1, keepdims=True)
    f_row = jnp.concatenate([f_low, f_high], axis=1)
    second_right = dot3(halves(jnp.broadcast_to(f_row, (8, 2 * HALF))), rt_split, NT)
    row = lax.broadcasted_iota(jnp.int32, (8, 128), 0)
    bbuf[0] = jnp.where(row == 0, second_right, right_square)
    ibx = net.slot()
    iby = [net.slot() for _ in range(ny)]
    net.send(ibx, bbuf.at[0], brecv, hi_peer)
    for o in near_first(nz)[: nz // 2]:
        gather2.over_x(o)
    net.arrive(ibx, brecv, hi_peer)
    bbuf[1] = bbuf[0] + brecv[...]
    for o in far_first(ny):
        net.send(iby[o], bbuf.at[1], byrecv.at[o], y_peer(o))
    for o in near_first(nz)[nz // 2 :]:
        gather2.over_x(o)
    whole = bbuf[1]
    for o in near_first(ny):
        net.arrive(iby[o], byrecv.at[o], y_peer(o))
        whole = whole + byrecv[o]
    norm_right = jnp.sqrt(whole[1:2, 0:1] + FLOOR)
    scaled = whole[0:1, :] / norm_right
    tops = jnp.sum(scaled * scaled, axis=1, keepdims=True)
    cbuf[0] = jnp.where(row == 0, tops, left_square)
    csum.over_core()
    for o in ([0] + near_first(nz))[: nz // 2]:
        gather2.over_core(o)
    csum.over_x()
    for o in ([0] + near_first(nz))[nz // 2 :]:
        gather2.over_core(o)
    csum.over_z()

    right_out[...] = rtile[...].T
    square[...] = jnp.zeros_like(square)
    square[pl.ds(0, 32), :] = lrow[:, old_lanes]
    square2[...] = square[...].T
    left_out[...] = square2[pl.ds(pl.multiple_of((a % 2) * SLAB, SLAB), SLAB), pl.ds(0, 32)]

    tops = csum.total()
    top_right = jnp.sqrt(tops[0:1, 0:1] + FLOOR)
    top_left = jnp.sqrt(tops[1:2, 0:1] + FLOOR)
    for o in [0] + near_first(nz):
        gather2.landed(o)
    mixed = 5.0 * grad[...] - prod[...] / top_right
    left_term = dot3(halves(lrow[...]), halves(mixed), NN)
    own32 = pl.ds(pl.multiple_of(dp * 32, 32), 32)
    own = 5.0 * grad[own32, :] - prod[own32, :] / top_right
    scale = lax.rsqrt(jnp.sqrt(top_left * top_right)) * 0.0625
    update_out[...] = (5.0 * own - left_term / top_left) * scale

    @pl.when(jnp.logical_not(on_diagonal))
    def _():
        net.copy(i_flip, gown, panel.at[flip_rows, :], flip_peer).wait_send()

    net.finish()


def step(nz, ny, ff, activations, grad_output, left_old, right_old, probe_left, probe_right):
    d_model = activations.shape[1]
    block = grad_output.shape[1]
    vmem = pltpu.VMEM

    def scatter_bufs():
        return [
            vmem((d_model, block), F32),
            vmem((d_model, HALF), F32),
            vmem((nz, SLAB, HALF), F32),
            vmem((nz, SLAB, HALF), F32),
            vmem((nz, SLAB, HALF), F32),
            vmem((nz, SLAB, HALF), F32),
            vmem((d_model, block), F32),
        ]

    scratch = [
        *scatter_bufs(),
        *scatter_bufs(),
        vmem((SLAB, HALF), F32),
        vmem((d_model, HALF), F32),
        vmem((HALF, block), F32),
        vmem((32, d_model), F32),
        vmem((ny, 32, 128), F32),
        vmem((32, 128), F32),
        vmem((32, 128), F32),
        vmem((32, d_model), F32),
        vmem((128, 128), F32),
        vmem((128, 128), F32),
        vmem((3, 16, 128), F32),
        vmem((2, 16, 128), F32),
        vmem((nz, 16, 128), F32),
        vmem((2, 8, 128), F32),
        vmem((8, 128), F32),
        vmem((ny, 8, 128), F32),
        vmem((3, 8, 128), F32),
        vmem((2, 8, 128), F32),
        vmem((nz, 8, 128), F32),
        pltpu.SemaphoreType.DMA((COPIES,)),
        pltpu.SemaphoreType.DMA((COPIES,)),
    ]
    spec = pl.BlockSpec(memory_space=pltpu.VMEM)
    return pl.pallas_call(
        functools.partial(kernel, nz, ny, ff),
        out_shape=(
            jax.ShapeDtypeStruct(left_old.shape, F32),
            jax.ShapeDtypeStruct(right_old.shape, F32),
            jax.ShapeDtypeStruct((d_model // (4 * nz), block), F32),
        ),
        in_specs=[spec] * 6,
        out_specs=(spec,) * 3,
        scratch_shapes=scratch,
        compiler_params=pltpu.CompilerParams(
            collective_id=0, has_side_effects=True, vmem_limit_bytes=48 * 1024 * 1024
        ),
        name="shampoo",
    )(
        activations,
        grad_output,
        left_old,
        right_old,
        probe_left.reshape(-1, 128),
        probe_right.reshape(-1, 128),
    )


def solution(mesh):
    nz = mesh.shape["dp"] // 4
    ny = mesh.shape["pre"]
    in_specs = (
        P("dp", None),
        P("dp", ("mp", "pre")),
        P(("mp", "pre"), "dp"),
        P(("mp", "pre"), "dp"),
        P(),
        P(),
    )
    out_specs = (P(("mp", "pre"), "dp"), P(("mp", "pre"), "dp"), P("dp", ("mp", "pre")))
    ff = 2 * ny * 2 * HALF
    return jax.shard_map(
        functools.partial(step, nz, ny, ff),
        mesh=mesh,
        in_specs=in_specs,
        out_specs=out_specs,
        check_vma=False,
    )
```

time: 462 us -> 101 us (0.22)
  waiting for transfers between devices: 194 us -> 0 us
  blocking collectives: 142 us -> 0 us
  Pallas kernels: 0 us -> 91.6 us
  starting transfers between devices: 66 us -> 0 us
  between operations: 17.8 us -> 0.65 us
  matrix products: 16.7 us -> 0 us
  other arithmetic: 9.4 us -> 0 us
  local copies, waits for them, and re-layouts: 14.8 us -> 8.08 us
    unnamed x2 -> x0, blocking collectives: 124 us -> none
    all_to_all x6 -> x0, waiting for transfers between devices: 107 us -> none  [the longest x2 56.1 us: sum_at_owner(): lax.all_to_all(tiles, axis, split_axis=0, concat_axis=0, tiled=True)]
    pallas_call x0 -> x1, Pallas kernels: none -> 91.6 us  [step(): pl.pallas_call(functools.partial(kernel, nz, ny, ff), out_shape=(jax.Shap...]
    all_gather x1 -> x0, waiting for transfers between devices: 87.2 us -> none  [picked(): lax.all_gather(shard, axis)]
    all_to_all x6 -> x0, starting transfers between devices: 65.9 us -> none  [the longest x4 38.1 us: sent_to_all(): lax.all_to_all(jnp.broadcast_to(shard[None], (devices, *shard.shape)), ax...]
    all_to_all x1 -> x0, blocking collectives: 18.3 us -> none  [sum_at_owner(): lax.all_to_all(tiles, axis, split_axis=0, concat_axis=0, tiled=True)]
    dot_general x9 -> x0, matrix products: 16.7 us -> none  [the longest x1 3.3 us: shards(): jnp.dot(step_panel, right_mix, precision=highest, preferred_element_type=...]
    reduce_sum x9 -> x0, other arithmetic: 5.32 us -> none  [the longest x3 2.62 us: sum_at_owner(): return arrived.sum(axis=0)]
  transfers between devices with their start and end apart: 8 -> 0, of which waited for: 7 -> 0; matrix products, arithmetic and copies ran while one was open for 5% -> 0% of each run, Pallas kernels for 0% -> 0%
where the time goes in v1:
time: 101 us; the launch traced here: 100 us
  Pallas kernels  91.6 us (91%)
  local copies, waits for them, and re-layouts  8.08 us (8%)
    pallas_call x1, Pallas kernels, step(): pl.pallas_call(functools.partial(kernel, nz, ny, ff), out_shape=(jax.Shap...  91.6 us
    unnamed x13, local copies, waits for them, and re-layouts  7.4 us

profile of v1, /device:TPU:1, one launch (start us, length us, event | category | flops | bytes accessed | tf_op | source)
XLA Modules:
  0.0 100.3 jit_solution(16926657024754088626)
XLA Ops:
  0.6 0.8 copy.9.left_old
  1.4 0.0 copy-start
  1.4 1.9 %copy-done = bf16[1536,1024]{1,0:T(8,128)(2,1)S(1)} copy-done((bf16[1536,1024]{1,0:T(8,128)(2,1)S(1)}, bf16[1536,1024]{1,0:T(8,128)(2,1)}, u32[]{:S(2)}) %copy-start) | copy-done | bytes 3145752
  3.3 0.0 copy-start.1
  3.3 1.1 %copy-done.1 = bf16[1536,256]{1,0:T(8,128)(2,1)S(1)} copy-done((bf16[1536,256]{1,0:T(8,128)(2,1)S(1)}, bf16[1536,256]{1,0:T(8,128)(2,1)}, u32[]{:S(2)}) %copy-start.1) | copy-done | bytes 786456
  4.5 0.0 copy-start.2
  4.5 0.9 copy-done.2
  5.4 0.0 copy-start.3
  5.4 0.7 copy-done.3
  6.1 0.0 copy-start.4
  6.1 0.7 copy-done.4
  6.8 91.6 %shampoo.1 = (f32[64,32]{1,0:T(8,128)S(1)}, f32[256,128]{1,0:T(8,128)S(1)}, f32[32,256]{1,0:T(8,128)S(1)}) custom-call(bf16[1536,1024]{1,0:T(8,128)(2,1)S(1)} %copy-done, bf16[1536,256]{1,0:T(8,128)(2,1)S(1)} %copy-done.1, f32[64,32]{1,0:T(8,128)S(1)} %copy.9.left_old, f32[256,128]{1,0:T(8,128)S(1)} %copy-done.2, f32[8,128]{1,0:T(8,128)S(1)} %bitcast.3, ...), custom_call_target="tpu_custom_call" | custom-call | tf_op jit(solution)/shard_map/shampoo/pallas_call | solution.py:529
  98.3 0.7 copy.10
  99.0 0.7 copy.13
  99.7 0.6 copy.14
Async XLA Ops:
  1.4 1.9 %copy-start = (bf16[1536,1024]{1,0:T(8,128)(2,1)S(1)}, bf16[1536,1024]{1,0:T(8,128)(2,1)}, u32[]{:S(2)}) copy-start(bf16[1536,1024]{1,0:T(8,128)(2,1)} %act.1) | copy-start | bytes 9437188
  3.3 1.1 %copy-start.1 = (bf16[1536,256]{1,0:T(8,128)(2,1)S(1)}, bf16[1536,256]{1,0:T(8,128)(2,1)}, u32[]{:S(2)}) copy-start(bf16[1536,256]{1,0:T(8,128)(2,1)} %dy.1) | copy-start | bytes 2359300
  4.5 0.9 copy-start.2
  5.4 0.7 copy-start.3
  6.1 0.7 copy-start.4

commit v2 on v1

v2 whole, which is shorter than its diff:
```python
import functools

import jax
import jax.numpy as jnp
from jax import lax
from jax.experimental import pallas as pl
from jax.experimental.pallas import tpu as pltpu
from jax.sharding import PartitionSpec as P

MESH = pl.DeviceIdType.MESH
F32 = jnp.float32
BF16 = jnp.bfloat16

DECAY = 0.9
FLOOR = 1e-06
SLAB = 64
HALF = 128
COPIES = 216

NN = (((1,), (0,)), ((), ()))
NT = (((1,), (1,)), ((), ()))
TN = (((0,), (0,)), ((), ()))


def far_first(n):
    return sorted(range(1, n), key=lambda o: -min(o, n - o))


def near_first(n):
    return sorted(range(1, n), key=lambda o: min(o, n - o))


def halves(v):
    high = v.astype(BF16)
    return high, (v - high.astype(F32)).astype(BF16)


def dot3(a, b, dims):
    (ah, al), (bh, bl) = a, b
    dot = functools.partial(lax.dot_general, dimension_numbers=dims, preferred_element_type=F32)
    return dot(ah, bh) + (dot(ah, bl) + dot(al, bh))


class Net:
    def __init__(self, send_sem, recv_sem):
        self.send_sem, self.recv_sem, self.used, self.sent = send_sem, recv_sem, 0, []

    def slot(self):
        self.used += 1
        assert self.used <= COPIES
        return self.used - 1

    def copy(self, i, src, dst, device):
        return pltpu.make_async_remote_copy(
            src_ref=src,
            dst_ref=dst,
            send_sem=self.send_sem.at[i],
            recv_sem=self.recv_sem.at[i],
            device_id=device,
            device_id_type=MESH,
        )

    def send(self, i, src, dst, device):
        copy = self.copy(i, src, dst, device)
        copy.start()
        self.sent.append(copy)

    def arrive(self, i, dst, device):
        self.copy(i, dst, dst, device).wait_recv()

    def finish(self):
        for copy in self.sent:
            copy.wait_send()


def kernel(
    nz,
    ny,
    ff,
    act_hbm,
    dy_hbm,
    left_hbm,
    right_hbm,
    p_left_hbm,
    p_right_hbm,
    left_out,
    right_out,
    update_out,
    act,
    dy,
    left_old,
    right_old,
    p_left,
    p_right,
    part,
    rc,
    xs,
    rx,
    zs,
    rz,
    grad,
    part2,
    rc2,
    xs2,
    rx2,
    zs2,
    rz2,
    prod,
    gown,
    panel,
    rtile,
    lpart,
    lr,
    lsum,
    lx,
    lrow,
    abuf,
    arecv,
    azrecv,
    hbuf,
    hrecv,
    hyrecv,
    fbuf,
    frecv,
    fzrecv,
    bbuf,
    brecv,
    byrecv,
    cbuf,
    crecv,
    czrecv,
    send_sem,
    recv_sem,
    load_sem,
):
    d_model = nz * 2 * SLAB
    rows_l = d_model // 128
    dp, mp, pre = lax.axis_index("dp"), lax.axis_index("mp"), lax.axis_index("pre")
    z, xl, c = dp // 4, (dp // 2) % 2, dp % 2
    a = mp * ny + pre
    b = z * 2 + xl
    core_peer = (dp + 1 - 2 * c, mp, pre)
    x_peer = (dp + 2 - 4 * xl, mp, pre)
    hi_peer = (dp, 1 - mp, pre)

    turn = (z - a // 2 + ny // 2 + nz) % nz
    goal_hi = jnp.where(xl == a % 2, mp, 1 - mp)
    flip_to = (a * 2 + c, goal_hi, (pre + turn) % ny)
    came = (z + pre - b % ny + ny // 2 + nz) % nz
    came_lo = jnp.where(mp == b // ny, xl, 1 - xl)
    flip_from = (came * 4 + came_lo * 2 + c, b // ny, b % ny)
    flip_to_2 = (a * 2 + c, 1 - goal_hi, (pre + turn) % ny)
    flip_from_2 = (came * 4 + (1 - came_lo) * 2 + c, b // ny, b % ny)

    def z_at(o):
        return (z + o) % nz

    def z_peer(o):
        return (z_at(o) * 4 + xl * 2 + c, mp, pre)

    def y_at(o):
        return (pre + o) % ny

    def y_peer(o):
        return (dp, mp, y_at(o))

    net = Net(send_sem, recv_sem)

    barrier = pltpu.get_barrier_semaphore()

    def greet(device):
        pl.semaphore_signal(barrier, inc=1, device_id=device, device_id_type=MESH)

    greet(core_peer)
    greet(x_peer)
    greet(hi_peer)
    for o in range(1, nz):
        greet(z_peer(o))
    for o in range(1, ny):
        greet(y_peer(o))

    greet(flip_from)
    greet(flip_from_2)

    loads = []

    def load(src, dst):
        copy = pltpu.make_async_copy(src, dst, load_sem.at[len(loads)])
        copy.start()
        loads.append(copy)
        return copy

    def act_cols(o):
        return pl.ds(pl.multiple_of(z_at(o) * 128, 128), 128)

    z_order = far_first(nz) + [0]
    dy_load = load(dy_hbm, dy)
    act_loads = [load(act_hbm.at[:, act_cols(o)], act.at[i]) for i, o in enumerate(z_order)]
    other_loads = [
        load(left_hbm, left_old),
        load(right_hbm, right_old),
        load(p_left_hbm, p_left),
        load(p_right_hbm, p_right),
    ]

    def slab_rows(z_, xl_):
        return pl.ds(pl.multiple_of((z_ * 2 + xl_) * SLAB, SLAB), SLAB)

    def pair_rows(z_):
        return pl.ds(pl.multiple_of(z_ * 2 * SLAB, 2 * SLAB), 2 * SLAB)

    def half_cols(c_):
        return pl.ds(pl.multiple_of(c_ * HALF, HALF), HALF)

    mine, other = half_cols(c), half_cols(1 - c)

    class Scatter:
        def __init__(self, part, rc, xs, rx, zs, rz):
            self.part, self.rc, self.xs, self.rx, self.zs, self.rz = part, rc, xs, rx, zs, rz
            self.ic = [net.slot() for _ in range(nz)]
            self.ix = [net.slot() for _ in range(nz)]
            self.iz = [net.slot() for _ in range(nz)]

        def block(self, o, value):
            rows = pair_rows(z_at(o))
            self.part[rows, :] = value
            net.send(self.ic[o], self.part.at[rows, other], self.rc.at[rows, :], core_peer)

        def over_x(self, o):
            rows = pair_rows(z_at(o))
            net.arrive(self.ic[o], self.rc.at[rows, :], core_peer)
            theirs = slab_rows(z_at(o), 1 - xl)
            self.xs[o] = self.part[theirs, mine] + self.rc[theirs, :]
            net.send(self.ix[o], self.xs.at[o], self.rx.at[o], x_peer)

        def over_z(self, o):
            net.arrive(self.ix[o], self.rx.at[o], x_peer)
            ours = slab_rows(z_at(o), xl)
            self.zs[o] = self.part[ours, mine] + self.rc[ours, :] + self.rx[o]
            if o:
                net.send(self.iz[o], self.zs.at[o], self.rz.at[o], z_peer(o))

        def total(self):
            value = self.zs[0]
            for o in near_first(nz):
                net.arrive(self.iz[o], self.rz.at[o], z_peer(o))
                value = value + self.rz[o]
            return value

    class Gather:
        def __init__(self, full):
            self.full = full
            self.ic = [net.slot() for _ in range(nz)]
            self.ix = [net.slot() for _ in range(nz)]
            self.iz = [net.slot() for _ in range(nz)]

        def over_z(self, value):
            rows = slab_rows(z, xl)
            self.full[rows, mine] = value
            chunk = self.full.at[rows, mine]
            for o in far_first(nz):
                net.send(self.iz[o], chunk, chunk, z_peer(o))
            net.send(self.ix[0], chunk, chunk, x_peer)

        def over_x(self, o):
            chunk = self.full.at[slab_rows(z_at(nz - o), xl), mine]
            net.arrive(self.iz[o], chunk, z_peer(nz - o))
            net.send(self.ix[o], chunk, chunk, x_peer)

        def over_core(self, o):
            z_ = z_at(nz - o)
            net.arrive(self.ix[o], self.full.at[slab_rows(z_, 1 - xl), mine], x_peer)
            pair = self.full.at[pair_rows(z_), mine]
            net.send(self.ic[o], pair, pair, core_peer)

        def landed(self, o):
            net.arrive(self.ic[o], self.full.at[pair_rows(z_at(nz - o)), other], core_peer)

    class Sum:
        def __init__(self, buf, recv, zrecv):
            self.buf, self.recv, self.zrecv = buf, recv, zrecv
            self.ic, self.ix = net.slot(), net.slot()
            self.iz = [net.slot() for _ in range(nz)]

        def over_core(self):
            net.send(self.ic, self.buf.at[0], self.recv.at[0], core_peer)

        def over_x(self):
            net.arrive(self.ic, self.recv.at[0], core_peer)
            self.buf[1] = self.buf[0] + self.recv[0]
            net.send(self.ix, self.buf.at[1], self.recv.at[1], x_peer)

        def over_z(self):
            net.arrive(self.ix, self.recv.at[1], x_peer)
            self.buf[2] = self.buf[1] + self.recv[1]
            for o in far_first(nz):
                net.send(self.iz[o], self.buf.at[2], self.zrecv.at[o], z_peer(o))

        def total(self):
            value = self.buf[2]
            for o in near_first(nz):
                net.arrive(self.iz[o], self.zrecv.at[o], z_peer(o))
                value = value + self.zrecv[o]
            return value

    class SumA:
        def __init__(self, buf, recv, yrecv):
            self.buf, self.recv, self.yrecv = buf, recv, yrecv
            self.ix = net.slot()
            self.iy = [net.slot() for _ in range(ny)]

        def over_hi(self):
            net.send(self.ix, self.buf.at[0], self.recv, hi_peer)

        def over_y(self):
            net.arrive(self.ix, self.recv, hi_peer)
            self.buf[1] = self.buf[0] + self.recv[...]
            for o in far_first(ny):
                net.send(self.iy[o], self.buf.at[1], self.yrecv.at[o], y_peer(o))

        def total(self):
            value = self.buf[1]
            for o in near_first(ny):
                net.arrive(self.iy[o], self.yrecv.at[o], y_peer(o))
                value = value + self.yrecv[o]
            return value

    old_sum = Sum(abuf, arecv, azrecv)
    h_sum = SumA(hbuf, hrecv, hyrecv)
    image_sum = SumA(bbuf, brecv, byrecv)
    left_sum = Sum(fbuf, frecv, fzrecv)
    last_sum = Sum(cbuf, crecv, czrecv)

    first = Scatter(part, rc, xs, rx, zs, rz)
    gather = Gather(grad)

    def grad_block(i):
        act_loads[i].wait()
        return lax.dot_general(act[i], dy[...], TN, preferred_element_type=F32)

    def blocks_and_x(scatter, block_of, between=()):
        between = dict(between)
        for i in range(nz):
            scatter.block(z_order[i], block_of(i))
            if i in between:
                between[i]()
            if i >= 3:
                scatter.over_x(z_order[i - 3])
        for i in range(nz - 3, nz):
            if i >= 0:
                scatter.over_x(z_order[i])

    dy_load.wait()
    first_value = grad_block(0)
    pl.semaphore_wait(barrier, 5 + (nz - 1) + (ny - 1))
    blocks_and_x(first, lambda i: grad_block(i) if i else first_value)

    for copy in other_loads:
        copy.wait()
    row = lax.broadcasted_iota(jnp.int32, (8, 128), 0)
    p_row = jnp.broadcast_to(p_right[pl.ds(dp, 1), :], (8, 128))
    old_right = dot3(halves(p_row), halves(right_old[...]), NT)
    abuf[0] = jnp.where(row == 0, old_right[:, :HALF], old_right[:, HALF:])
    old_sum.over_core()
    for o in z_order[: nz // 2]:
        first.over_z(o)
    old_sum.over_x()
    for o in z_order[nz // 2 :]:
        first.over_z(o)
    old_sum.over_z()
    gown[...] = first.total()

    i_flip, i_flip_2 = net.slot(), net.slot()
    iy = [net.slot() for _ in range(ny)]
    ih = [net.slot() for _ in range(ny)]

    def panel_z(y_):
        return (z + y_ - b % ny + ny // 2 + nz) % nz

    def panel_slab(mp_, y_):
        return panel.at[slab_rows(panel_z(y_), jnp.where(mp_ == b // ny, xl, 1 - xl)), :]

    chunk = panel.at[slab_rows(z, xl), :]
    net.send(i_flip, gown, chunk, flip_to)
    net.send(i_flip_2, gown, chunk, flip_to_2)
    gather.over_z(gown[...])
    far = [o for o in far_first(ny) if min(o, ny - o) > 2]
    near = [o for o in far_first(ny) if min(o, ny - o) <= 2]
    net.arrive(i_flip, panel_slab(mp, pre), flip_from)
    for o in far:
        net.send(iy[o], panel_slab(mp, pre), panel_slab(mp, pre), y_peer(o))
    net.arrive(i_flip_2, panel_slab(1 - mp, pre), flip_from_2)
    own_pair = panel.at[pair_rows(panel_z(pre)), :]
    for o in near:
        net.send(iy[o], own_pair, own_pair, y_peer(o))
    for o in near_first(nz):
        gather.over_x(o)
    for o in reversed(far):
        slab = panel_slab(mp, y_at(ny - o))
        net.arrive(iy[o], slab, y_peer(ny - o))
        net.send(ih[o], slab, slab, hi_peer)
    for o in [0] + near_first(nz):
        gather.over_core(o)
    for o in [0] + near_first(nz):
        gather.landed(o)

    il = [net.slot() for _ in range(ny)]
    ilx = net.slot()
    ilg = [net.slot() for _ in range(ny)]
    own32 = pl.ds(pl.multiple_of(dp * 32, 32), 32)
    grad_split = halves(grad[...])
    probe_a = jnp.concatenate([p_right[pl.ds(2 * a, 1), :], p_right[pl.ds(2 * a + 1, 1), :]], axis=1)
    rows40 = jnp.concatenate([grad[own32, :], jnp.broadcast_to(probe_a, (8, 2 * HALF))], axis=0)
    both = dot3(halves(rows40), grad_split, NT)
    for j in range(rows_l):
        hbuf[0, pl.ds(j, 1), :] = both[32:33, j * 128 : (j + 1) * 128]
    h_sum.over_hi()
    lpart[...] = both[0:32, :] * (1.0 / ff)
    old_lanes = pl.ds(pl.multiple_of((a // 2) * 128, 128), 128)
    old = left_old[...] * DECAY
    side = lax.broadcasted_iota(jnp.int32, (32, 128), 1) // SLAB
    lpart[:, old_lanes] += jnp.where(side == a % 2, jnp.concatenate([old, old], axis=1), 0.0)

    def l_lanes(y_):
        return pl.ds(pl.multiple_of(y_ * 128, 128), 128)

    for o in far_first(ny):
        net.send(il[o], lpart.at[:, l_lanes(y_at(o))], lr.at[o], y_peer(o))
    for o in near:
        net.arrive(iy[o], panel.at[pair_rows(panel_z(y_at(ny - o))), :], y_peer(ny - o))
    h_sum.over_y()
    for o in reversed(far):
        net.arrive(ih[o], panel_slab(1 - mp, y_at(ny - o)), hi_peer)

    gram = dot3(halves(panel[...].T), grad_split, NN)
    rtile[...] = right_old[...].T * DECAY + gram * (1.0 / d_model)
    rt_split = halves(rtile[...])

    second = Scatter(part2, rc2, xs2, rx2, zs2, rz2)
    gather2 = Gather(prod)

    def prod_block(i):
        return dot3(halves(panel[pair_rows(z_at(z_order[i])), :]), rt_split, NN)

    def right_images():
        h = h_sum.total()
        h_row = jnp.concatenate([h[j : j + 1, :] for j in range(rows_l)], axis=1)
        new = dot3(halves(jnp.broadcast_to(h_row, (8, d_model))), grad_split, NN)
        old_image = old_sum.total()
        f_old = jnp.concatenate([old_image[0:1, :], old_image[1:2, :]], axis=1)
        f_row = f_old * DECAY + new[0:1, :] * (1.0 / d_model)
        square = jnp.sum(f_row * f_row, axis=1, keepdims=True)
        image = dot3(halves(jnp.broadcast_to(f_row, (8, 2 * HALF))), rt_split, NT)
        bbuf[0] = jnp.where(row == 0, image, square)
        image_sum.over_hi()

    def left_rows():
        total = lpart[:, l_lanes(pre)]
        for o in near_first(ny):
            net.arrive(il[o], lr.at[o], y_peer(o))
            total = total + lr[o]
        lsum[...] = total
        net.send(ilx, lsum, lx, hi_peer)

    blocks_and_x(second, prod_block, {min(3, nz - 1): right_images, nz - 1: left_rows})
    image_sum.over_y()
    net.arrive(ilx, lx, hi_peer)
    lrow[:, l_lanes(pre)] = lsum[...] + lx[...]
    own_lanes = lrow.at[:, l_lanes(pre)]
    for o in far_first(ny):
        net.send(ilg[o], own_lanes, own_lanes, y_peer(o))
    for o in z_order:
        second.over_z(o)

    whole = image_sum.total()
    norm_right = jnp.sqrt(whole[1:2, 0:1] + FLOOR)
    scaled = whole[0:1, :] / norm_right
    right_part = jnp.sum(scaled * scaled, axis=1, keepdims=True)
    cbuf[0] = jnp.broadcast_to(right_part, (8, 128))
    last_sum.over_core()

    for o in near_first(ny):
        net.arrive(ilg[o], lrow.at[:, l_lanes(y_at(ny - o))], y_peer(ny - o))
    last_sum.over_x()
    f_left = jnp.zeros((32, 1), F32)
    for j in range(rows_l):
        f_left = f_left + jnp.sum(
            lrow[:, j * 128 : (j + 1) * 128] * p_left[pl.ds(j, 1), :], axis=1, keepdims=True
        )
    left_image = jnp.sum(lrow[...] * f_left, axis=0, keepdims=True)
    for j in range(rows_l):
        fbuf[0, pl.ds(j, 1), :] = left_image[:, j * 128 : (j + 1) * 128]
    left_square = jnp.sum(f_left * f_left, axis=0, keepdims=True)
    fbuf[0, pl.ds(rows_l, 8), :] = jnp.broadcast_to(left_square, (8, 128))
    left_sum.over_core()
    last_sum.over_z()
    left_sum.over_x()

    gather2.over_z(second.total())
    left_sum.over_z()

    left_grad = dot3(halves(lrow[...]), grad_split, NN)
    right_out[...] = rtile[...].T
    lanes = lrow[:, old_lanes]
    left_out[...] = jnp.where(a % 2 == 0, lanes[:, :SLAB], lanes[:, SLAB:])
    for o in near_first(nz):
        gather2.over_x(o)
    for o in [0] + near_first(nz):
        gather2.over_core(o)
    top_right = jnp.sqrt(last_sum.total()[0:1, 0:1] + FLOOR)
    images = left_sum.total()
    norm_left = jnp.sqrt(images[rows_l : rows_l + 1, 0:1] + FLOOR)
    unit_image = images[0:rows_l, :] / norm_left
    top_left = jnp.sqrt(
        jnp.sum(jnp.sum(unit_image * unit_image, axis=1, keepdims=True), axis=0, keepdims=True)
        + FLOOR
    )
    scale = lax.rsqrt(jnp.sqrt(top_left * top_right)) * 0.0625
    left_prod = jnp.zeros_like(left_grad)
    for o in [0] + near_first(nz):
        gather2.landed(o)
        z_ = z_at(nz - o)
        left_prod = left_prod + dot3(
            halves(lrow[:, l_lanes(z_)]), halves(prod[pair_rows(z_), :]), NN
        )
    own = 5.0 * grad[own32, :] - prod[own32, :] / top_right
    left_term = 5.0 * left_grad - left_prod / top_right
    update_out[...] = (5.0 * own - left_term / top_left) * scale

    net.finish()


def store(left, right, update, left_out, right_out, update_out, sem):
    pairs = ((left, left_out), (right, right_out), (update, update_out))
    copies = [pltpu.make_async_copy(src, dst, sem.at[i]) for i, (src, dst) in enumerate(pairs)]
    for copy in copies:
        copy.start()
    for copy in copies:
        copy.wait()


def step(nz, ny, ff, activations, grad_output, left_old, right_old, probe_left, probe_right):
    d_model = activations.shape[1]
    block = grad_output.shape[1]
    rows_l = d_model // 128
    vmem = pltpu.VMEM

    def scatter_bufs():
        return [
            vmem((d_model, block), F32),
            vmem((d_model, HALF), F32),
            vmem((nz, SLAB, HALF), F32),
            vmem((nz, SLAB, HALF), F32),
            vmem((nz, SLAB, HALF), F32),
            vmem((nz, SLAB, HALF), F32),
            vmem((d_model, block), F32),
        ]

    scratch = [
        vmem((nz, activations.shape[0], 128), BF16),
        vmem(grad_output.shape, BF16),
        vmem((left_old.shape[1], left_old.shape[0]), F32),
        vmem(right_old.shape, F32),
        vmem((probe_left.shape[0] // 128, 128), F32),
        vmem((probe_right.shape[0] // 128, 128), F32),
        *scatter_bufs(),
        *scatter_bufs(),
        vmem((SLAB, HALF), F32),
        vmem((d_model, HALF), F32),
        vmem((HALF, block), F32),
        vmem((32, d_model), F32),
        vmem((ny, 32, 128), F32),
        vmem((32, 128), F32),
        vmem((32, 128), F32),
        vmem((32, d_model), F32),
        vmem((3, 8, 128), F32),
        vmem((2, 8, 128), F32),
        vmem((nz, 8, 128), F32),
        vmem((2, rows_l, 128), F32),
        vmem((rows_l, 128), F32),
        vmem((ny, rows_l, 128), F32),
        vmem((3, rows_l + 8, 128), F32),
        vmem((2, rows_l + 8, 128), F32),
        vmem((nz, rows_l + 8, 128), F32),
        vmem((2, 8, 128), F32),
        vmem((8, 128), F32),
        vmem((ny, 8, 128), F32),
        vmem((3, 8, 128), F32),
        vmem((2, 8, 128), F32),
        vmem((nz, 8, 128), F32),
        pltpu.SemaphoreType.DMA((COPIES,)),
        pltpu.SemaphoreType.DMA((COPIES,)),
        pltpu.SemaphoreType.DMA((nz + 5,)),
    ]
    spec = pl.BlockSpec(memory_space=pltpu.VMEM)
    left, right, update = pl.pallas_call(
        functools.partial(kernel, nz, ny, ff),
        out_shape=(
            jax.ShapeDtypeStruct((left_old.shape[1], left_old.shape[0]), F32),
            jax.ShapeDtypeStruct(right_old.shape, F32),
            jax.ShapeDtypeStruct((d_model // (4 * nz), block), F32),
        ),
        in_specs=[pl.BlockSpec(memory_space=pltpu.HBM)] * 6,
        out_specs=(spec,) * 3,
        scratch_shapes=scratch,
        compiler_params=pltpu.CompilerParams(
            collective_id=0, has_side_effects=True, vmem_limit_bytes=58 * 1024 * 1024
        ),
        name="shampoo",
    )(
        activations,
        grad_output,
        left_old.T,
        right_old,
        probe_left.reshape(-1, 128),
        probe_right.reshape(-1, 128),
    )
    left, right, update = pl.pallas_call(
        store,
        out_shape=tuple(jax.ShapeDtypeStruct(r.shape, F32) for r in (left, right, update)),
        in_specs=[spec] * 3,
        out_specs=(pl.BlockSpec(memory_space=pltpu.HBM),) * 3,
        scratch_shapes=[pltpu.SemaphoreType.DMA((3,))],
        name="store",
    )(left, right, update)
    return left.T, right, update


def solution(mesh):
    nz = mesh.shape["dp"] // 4
    ny = mesh.shape["pre"]
    in_specs = (
        P("dp", None),
        P("dp", ("mp", "pre")),
        P(("mp", "pre"), "dp"),
        P(("mp", "pre"), "dp"),
        P(),
        P(),
    )
    out_specs = (P(("mp", "pre"), "dp"), P(("mp", "pre"), "dp"), P("dp", ("mp", "pre")))
    ff = 2 * ny * 2 * HALF
    return jax.shard_map(
        functools.partial(step, nz, ny, ff),
        mesh=mesh,
        in_specs=in_specs,
        out_specs=out_specs,
        check_vma=False,
    )
```

time: 101 us -> 91.6 us (0.907)
  local copies, waits for them, and re-layouts: 8.08 us -> 0 us
    unnamed x13 -> x0, local copies, waits for them, and re-layouts: 7.4 us -> none
    pallas_call x1, Pallas kernels: 91.6 us -> 89.1 us  [step(): pl.pallas_call(functools.partial(kernel, nz, ny, ff), out_shape=(jax.Shap...]
    pallas_call x0 -> x1, Pallas kernels: none -> 1.59 us  [step(): pl.pallas_call(store, out_shape=tuple((jax.ShapeDtypeStruct(r.shape, F32)...]
where the time goes in v2:
time: 91.6 us; the launch traced here: 91.3 us
  Pallas kernels  90.7 us (99%)
    pallas_call x1, Pallas kernels, step(): pl.pallas_call(functools.partial(kernel, nz, ny, ff), out_shape=(jax.Shap...  89.1 us

profile of v2, /device:TPU:1, one launch (start us, length us, event | category | flops | bytes accessed | tf_op | source)
XLA Modules:
  0.0 91.3 jit_solution(11547696293858091916)
XLA Ops:
  0.6 89.1 %shampoo.1 = (f32[32,64]{1,0:T(8,128)}, f32[256,128]{1,0:T(8,128)}, f32[32,256]{1,0:T(8,128)}) custom-call(bf16[1536,1024]{1,0:T(8,128)(2,1)} %act_hbm.1, bf16[1536,256]{1,0:T(8,128)(2,1)} %dy_hbm.1, f32[32,64]{1,0:T(8,128)} %bitcast.4, f32[256,128]{1,0:T(8,128)} %right_hbm.1, f32[8,128]{1,0:T(8,128)} %bitcast.6, f32[32,128]{1,0:T(8,128)} %bitcast.5), custom_call_target="tpu_custom_call" | custom-call | tf_op jit(solution)/shard_map/shampoo/pallas_call | solution.py:596
  89.7 1.6 %store.1 = (f32[32,64]{1,0:T(8,128)}, f32[256,128]{1,0:T(8,128)}, f32[32,256]{1,0:T(8,128)}) custom-call(f32[32,64]{1,0:T(8,128)} %get-tuple-element.9.left, f32[256,128]{1,0:T(8,128)} %get-tuple-element.10.right, f32[32,256]{1,0:T(8,128)} %get-tuple-element.11.update), custom_call_target="tpu_custom_call" | custom-call | tf_op jit(solution)/shard_map/store/pallas_call | solution.py:618

commit v3 on v2

--- a/solution.py
+++ b/solution.py
@@ -171,17 +171,6 @@
     def greet(device):
         pl.semaphore_signal(barrier, inc=1, device_id=device, device_id_type=MESH)
 
-    greet(core_peer)
-    greet(x_peer)
-    greet(hi_peer)
-    for o in range(1, nz):
-        greet(z_peer(o))
-    for o in range(1, ny):
-        greet(y_peer(o))
-
-    greet(flip_from)
-    greet(flip_from_2)
-
     loads = []
 
     def load(src, dst):
@@ -203,6 +192,17 @@
         load(p_right_hbm, p_right),
     ]
 
+    greet(core_peer)
+    greet(x_peer)
+    greet(hi_peer)
+    for o in range(1, nz):
+        greet(z_peer(o))
+    for o in range(1, ny):
+        greet(y_peer(o))
+
+    greet(flip_from)
+    greet(flip_from_2)
+
     def slab_rows(z_, xl_):
         return pl.ds(pl.multiple_of((z_ * 2 + xl_) * SLAB, SLAB), SLAB)
 
@@ -258,9 +258,9 @@
             rows = slab_rows(z, xl)
             self.full[rows, mine] = value
             chunk = self.full.at[rows, mine]
-            for o in far_first(nz):
+            net.send(self.ix[0], chunk, chunk, x_peer)
+            for o in near_first(nz):
                 net.send(self.iz[o], chunk, chunk, z_peer(o))
-            net.send(self.ix[0], chunk, chunk, x_peer)
 
         def over_x(self, o):
             chunk = self.full.at[slab_rows(z_at(nz - o), xl), mine]
@@ -395,11 +395,14 @@
         net.send(iy[o], own_pair, own_pair, y_peer(o))
     for o in near_first(nz):
         gather.over_x(o)
+    core_order = [0] + near_first(nz)
+    for o in core_order[: nz // 2 + 1]:
+        gather.over_core(o)
     for o in reversed(far):
         slab = panel_slab(mp, y_at(ny - o))
         net.arrive(iy[o], slab, y_peer(ny - o))
         net.send(ih[o], slab, slab, hi_peer)
-    for o in [0] + near_first(nz):
+    for o in core_order[nz // 2 + 1 :]:
         gather.over_core(o)
     for o in [0] + near_first(nz):
         gather.landed(o)
@@ -428,13 +431,13 @@
         net.send(il[o], lpart.at[:, l_lanes(y_at(o))], lr.at[o], y_peer(o))
     for o in near:
         net.arrive(iy[o], panel.at[pair_rows(panel_z(y_at(ny - o))), :], y_peer(ny - o))
-    h_sum.over_y()
     for o in reversed(far):
         net.arrive(ih[o], panel_slab(1 - mp, y_at(ny - o)), hi_peer)
 
     gram = dot3(halves(panel[...].T), grad_split, NN)
     rtile[...] = right_old[...].T * DECAY + gram * (1.0 / d_model)
     rt_split = halves(rtile[...])
+    h_sum.over_y()
 
     second = Scatter(part2, rc2, xs2, rx2, zs2, rz2)
     gather2 = Gather(prod)
@@ -462,26 +465,27 @@
         lsum[...] = total
         net.send(ilx, lsum, lx, hi_peer)
 
-    blocks_and_x(second, prod_block, {min(3, nz - 1): right_images, nz - 1: left_rows})
-    image_sum.over_y()
+    blocks_and_x(second, prod_block)
+    left_rows()
+    cut = [1, 3, 6] if nz > 6 else [1, 1, 1]
+    for o in z_order[: cut[0]]:
+        second.over_z(o)
+    right_images()
+    for o in z_order[cut[0] : cut[1]]:
+        second.over_z(o)
     net.arrive(ilx, lx, hi_peer)
     lrow[:, l_lanes(pre)] = lsum[...] + lx[...]
     own_lanes = lrow.at[:, l_lanes(pre)]
     for o in far_first(ny):
         net.send(ilg[o], own_lanes, own_lanes, y_peer(o))
-    for o in z_order:
+    for o in z_order[cut[1] : cut[2]]:
         second.over_z(o)
-
-    whole = image_sum.total()
-    norm_right = jnp.sqrt(whole[1:2, 0:1] + FLOOR)
-    scaled = whole[0:1, :] / norm_right
-    right_part = jnp.sum(scaled * scaled, axis=1, keepdims=True)
-    cbuf[0] = jnp.broadcast_to(right_part, (8, 128))
-    last_sum.over_core()
+    image_sum.over_y()
+    for o in z_order[cut[2] :]:
+        second.over_z(o)
 
     for o in near_first(ny):
         net.arrive(ilg[o], lrow.at[:, l_lanes(y_at(ny - o))], y_peer(ny - o))
-    last_sum.over_x()
     f_left = jnp.zeros((32, 1), F32)
     for j in range(rows_l):
         f_left = f_left + jnp.sum(
@@ -493,17 +497,27 @@
     left_square = jnp.sum(f_left * f_left, axis=0, keepdims=True)
     fbuf[0, pl.ds(rows_l, 8), :] = jnp.broadcast_to(left_square, (8, 128))
     left_sum.over_core()
-    last_sum.over_z()
+
+    gather2.over_z(second.total())
     left_sum.over_x()
 
-    gather2.over_z(second.total())
-    left_sum.over_z()
+    whole = image_sum.total()
+    norm_right = jnp.sqrt(whole[1:2, 0:1] + FLOOR)
+    scaled = whole[0:1, :] / norm_right
+    right_part = jnp.sum(scaled * scaled, axis=1, keepdims=True)
+    cbuf[0] = jnp.broadcast_to(right_part, (8, 128))
+    last_sum.over_core()
 
     left_grad = dot3(halves(lrow[...]), grad_split, NN)
     right_out[...] = rtile[...].T
     lanes = lrow[:, old_lanes]
     left_out[...] = jnp.where(a % 2 == 0, lanes[:, :SLAB], lanes[:, SLAB:])
-    for o in near_first(nz):
+    last_sum.over_x()
+    left_sum.over_z()
+    for o in near_first(nz)[:2]:
+        gather2.over_x(o)
+    last_sum.over_z()
+    for o in near_first(nz)[2:]:
         gather2.over_x(o)
     for o in [0] + near_first(nz):
         gather2.over_core(o)

time: 91.6 us -> 86.5 us (0.944)
  Pallas kernels: 90.7 us -> 85.7 us
    pallas_call x1, Pallas kernels: 89.1 us -> 84.1 us  [step(): pl.pallas_call(functools.partial(kernel, nz, ny, ff), out_shape=(jax.Shap...]
where the time goes in v3:
time: 86.5 us; the launch traced here: 86.4 us
  Pallas kernels  85.7 us (99%)
    pallas_call x1, Pallas kernels, step(): pl.pallas_call(functools.partial(kernel, nz, ny, ff), out_shape=(jax.Shap...  84.1 us

profile of v3, /device:TPU:1, one launch (start us, length us, event | category | flops | bytes accessed | tf_op | source)
XLA Modules:
  0.0 86.4 jit_solution(7135628441287998196)
XLA Ops:
  0.6 84.1 %shampoo.1 = (f32[32,64]{1,0:T(8,128)}, f32[256,128]{1,0:T(8,128)}, f32[32,256]{1,0:T(8,128)}) custom-call(bf16[1536,1024]{1,0:T(8,128)(2,1)} %act_hbm.1, bf16[1536,256]{1,0:T(8,128)(2,1)} %dy_hbm.1, f32[32,64]{1,0:T(8,128)} %bitcast.4, f32[256,128]{1,0:T(8,128)} %right_hbm.1, f32[8,128]{1,0:T(8,128)} %bitcast.6, f32[32,128]{1,0:T(8,128)} %bitcast.5), custom_call_target="tpu_custom_call" | custom-call | tf_op jit(solution)/shard_map/shampoo/pallas_call | solution.py:610
  84.8 1.6 %store.1 = (f32[32,64]{1,0:T(8,128)}, f32[256,128]{1,0:T(8,128)}, f32[32,256]{1,0:T(8,128)}) custom-call(f32[32,64]{1,0:T(8,128)} %get-tuple-element.9.left, f32[256,128]{1,0:T(8,128)} %get-tuple-element.10.right, f32[32,256]{1,0:T(8,128)} %get-tuple-element.11.update), custom_call_target="tpu_custom_call" | custom-call | tf_op jit(solution)/shard_map/store/pallas_call | solution.py:632

commit v4 on v3

--- a/solution.py
+++ b/solution.py
@@ -114,6 +114,12 @@
     lsum,
     lx,
     lrow,
+    lrows,
+    terms,
+    xterm,
+    sums,
+    cterm,
+    wrow,
     abuf,
     arecv,
     azrecv,
@@ -247,6 +253,8 @@
                 value = value + self.rz[o]
             return value
 
+    mixed = near_first(nz)[:2] + [o for o in far_first(nz) if o not in near_first(nz)[:2]]
+
     class Gather:
         def __init__(self, full):
             self.full = full
@@ -259,7 +267,7 @@
             self.full[rows, mine] = value
             chunk = self.full.at[rows, mine]
             net.send(self.ix[0], chunk, chunk, x_peer)
-            for o in near_first(nz):
+            for o in mixed:
                 net.send(self.iz[o], chunk, chunk, z_peer(o))
 
         def over_x(self, o):
@@ -362,6 +370,8 @@
     old_right = dot3(halves(p_row), halves(right_old[...]), NT)
     abuf[0] = jnp.where(row == 0, old_right[:, :HALF], old_right[:, HALF:])
     old_sum.over_core()
+    for z_ in range(nz):
+        prod[slab_rows(z_, 1 - xl), :] = jnp.zeros((SLAB, HALF), F32)
     for o in z_order[: nz // 2]:
         first.over_z(o)
     old_sum.over_x()
@@ -393,9 +403,9 @@
     own_pair = panel.at[pair_rows(panel_z(pre)), :]
     for o in near:
         net.send(iy[o], own_pair, own_pair, y_peer(o))
-    for o in near_first(nz):
+    for o in mixed:
         gather.over_x(o)
-    core_order = [0] + near_first(nz)
+    core_order = [0] + mixed
     for o in core_order[: nz // 2 + 1]:
         gather.over_core(o)
     for o in reversed(far):
@@ -404,7 +414,7 @@
         net.send(ih[o], slab, slab, hi_peer)
     for o in core_order[nz // 2 + 1 :]:
         gather.over_core(o)
-    for o in [0] + near_first(nz):
+    for o in core_order:
         gather.landed(o)
 
     il = [net.slot() for _ in range(ny)]
@@ -440,7 +450,6 @@
     h_sum.over_y()
 
     second = Scatter(part2, rc2, xs2, rx2, zs2, rz2)
-    gather2 = Gather(prod)
 
     def prod_block(i):
         return dot3(halves(panel[pair_rows(z_at(z_order[i])), :]), rt_split, NN)
@@ -467,7 +476,7 @@
 
     blocks_and_x(second, prod_block)
     left_rows()
-    cut = [1, 3, 6] if nz > 6 else [1, 1, 1]
+    cut = [4, 5] if nz > 5 else [1, 1]
     for o in z_order[: cut[0]]:
         second.over_z(o)
     right_images()
@@ -478,14 +487,20 @@
     own_lanes = lrow.at[:, l_lanes(pre)]
     for o in far_first(ny):
         net.send(ilg[o], own_lanes, own_lanes, y_peer(o))
-    for o in z_order[cut[1] : cut[2]]:
+    for o in z_order[cut[1] :]:
         second.over_z(o)
     image_sum.over_y()
-    for o in z_order[cut[2] :]:
-        second.over_z(o)
 
     for o in near_first(ny):
         net.arrive(ilg[o], lrow.at[:, l_lanes(y_at(ny - o))], y_peer(ny - o))
+
+    def l_rows(xl_, c_):
+        return lrows.at[pl.ds(pl.multiple_of((xl_ * 2 + c_) * 32, 32), 32), :]
+
+    i_rows, i_rows_x, i_rows_xc = net.slot(), net.slot(), net.slot()
+    net.send(i_rows_x, lrow, l_rows(xl, c), x_peer)
+    net.send(i_rows, lrow, l_rows(xl, c), core_peer)
+    l_rows(xl, c)[...] = lrow[...]
     f_left = jnp.zeros((32, 1), F32)
     for j in range(rows_l):
         f_left = f_left + jnp.sum(
@@ -498,7 +513,17 @@
     fbuf[0, pl.ds(rows_l, 8), :] = jnp.broadcast_to(left_square, (8, 128))
     left_sum.over_core()
 
-    gather2.over_z(second.total())
+    iz2 = [net.slot() for _ in range(nz)]
+    i_prod, i_term_x, i_term_c = net.slot(), net.slot(), net.slot()
+    prod[slab_rows(z, xl), :] = second.total()
+    own_prod = prod.at[slab_rows(z, xl), :]
+    for o in far_first(nz):
+        net.send(iz2[o], own_prod, own_prod, z_peer(o))
+
+    def rows_of(c_):
+        return pl.ds(pl.multiple_of((z * 2 + xl) * SLAB + c_ * 32, 32), 32)
+
+    net.send(i_prod, prod.at[rows_of(1 - c), :], wrow, core_peer)
     left_sum.over_x()
 
     whole = image_sum.total()
@@ -514,13 +539,26 @@
     left_out[...] = jnp.where(a % 2 == 0, lanes[:, :SLAB], lanes[:, SLAB:])
     last_sum.over_x()
     left_sum.over_z()
-    for o in near_first(nz)[:2]:
-        gather2.over_x(o)
     last_sum.over_z()
-    for o in near_first(nz)[2:]:
-        gather2.over_x(o)
-    for o in [0] + near_first(nz):
-        gather2.over_core(o)
+    net.arrive(i_rows_x, l_rows(1 - xl, c), x_peer)
+    net.send(i_rows_xc, l_rows(1 - xl, c), l_rows(1 - xl, c), core_peer)
+    net.arrive(i_rows, l_rows(xl, 1 - c), core_peer)
+    net.arrive(i_rows_xc, l_rows(1 - xl, 1 - c), core_peer)
+
+    term = jnp.zeros((128, HALF), F32)
+    for o in [0] + [nz - o for o in far_first(nz)]:
+        z_ = z_at(o)
+        if o:
+            net.arrive(iz2[nz - o], prod.at[slab_rows(z_, xl), :], z_peer(o))
+        term = term + dot3(
+            halves(lrows[:, l_lanes(z_)]), halves(prod[pair_rows(z_), :]), NN
+        )
+    terms[...] = term
+
+    def term_rows(xl_):
+        return pl.ds(pl.multiple_of(xl_ * SLAB, SLAB), SLAB)
+
+    net.send(i_term_x, terms.at[term_rows(1 - xl), :], xterm, x_peer)
     top_right = jnp.sqrt(last_sum.total()[0:1, 0:1] + FLOOR)
     images = left_sum.total()
     norm_left = jnp.sqrt(images[rows_l : rows_l + 1, 0:1] + FLOOR)
@@ -530,16 +568,21 @@
         + FLOOR
     )
     scale = lax.rsqrt(jnp.sqrt(top_left * top_right)) * 0.0625
-    left_prod = jnp.zeros_like(left_grad)
-    for o in [0] + near_first(nz):
-        gather2.landed(o)
-        z_ = z_at(nz - o)
-        left_prod = left_prod + dot3(
-            halves(lrow[:, l_lanes(z_)]), halves(prod[pair_rows(z_), :]), NN
-        )
-    own = 5.0 * grad[own32, :] - prod[own32, :] / top_right
-    left_term = 5.0 * left_grad - left_prod / top_right
-    update_out[...] = (5.0 * own - left_term / top_left) * scale
+    rest = 5.0 * (5.0 * grad[own32, :] - left_grad / top_left)
+    net.arrive(i_term_x, xterm, x_peer)
+    sums[...] = terms[term_rows(xl), :] + xterm[...]
+
+    def sum_rows(c_):
+        return pl.ds(pl.multiple_of(c_ * 32, 32), 32)
+
+    net.send(i_term_c, sums.at[sum_rows(1 - c), :], cterm, core_peer)
+    update_out[...] = rest
+    by_right = (sums[sum_rows(c), :] / top_left - 5.0 * prod[rows_of(c), :]) / top_right
+    update_out[:, mine] = (update_out[:, mine] + by_right) * scale
+    net.arrive(i_prod, wrow, core_peer)
+    net.arrive(i_term_c, cterm, core_peer)
+    by_right = (cterm[...] / top_left - 5.0 * wrow[...]) / top_right
+    update_out[:, other] = (update_out[:, other] + by_right) * scale
 
     net.finish()
 
@@ -559,7 +602,7 @@
     rows_l = d_model // 128
     vmem = pltpu.VMEM
 
-    def scatter_bufs():
+    def scatter_bufs(columns):
         return [
             vmem((d_model, block), F32),
             vmem((d_model, HALF), F32),
@@ -567,7 +610,7 @@
             vmem((nz, SLAB, HALF), F32),
             vmem((nz, SLAB, HALF), F32),
             vmem((nz, SLAB, HALF), F32),
-            vmem((d_model, block), F32),
+            vmem((d_model, columns), F32),
         ]
 
     scratch = [
@@ -577,8 +620,8 @@
         vmem(right_old.shape, F32),
         vmem((probe_left.shape[0] // 128, 128), F32),
         vmem((probe_right.shape[0] // 128, 128), F32),
-        *scatter_bufs(),
-        *scatter_bufs(),
+        *scatter_bufs(block),
+        *scatter_bufs(HALF),
         vmem((SLAB, HALF), F32),
         vmem((d_model, HALF), F32),
         vmem((HALF, block), F32),
@@ -587,6 +630,12 @@
         vmem((32, 128), F32),
         vmem((32, 128), F32),
         vmem((32, d_model), F32),
+        vmem((128, d_model), F32),
+        vmem((128, HALF), F32),
+        vmem((SLAB, HALF), F32),
+        vmem((SLAB, HALF), F32),
+        vmem((32, HALF), F32),
+        vmem((32, HALF), F32),
         vmem((3, 8, 128), F32),
         vmem((2, 8, 128), F32),
         vmem((nz, 8, 128), F32),

time: 86.5 us -> 83.8 us (0.969)
  Pallas kernels: 85.7 us -> 83 us
    pallas_call x1, Pallas kernels: 84.1 us -> 81.4 us  [step(): pl.pallas_call(functools.partial(kernel, nz, ny, ff), out_shape=(jax.Shap...]
where the time goes in v4:
time: 83.8 us; the launch traced here: 83.7 us
  Pallas kernels  83 us (99%)
    pallas_call x1, Pallas kernels, step(): pl.pallas_call(functools.partial(kernel, nz, ny, ff), out_shape=(jax.Shap...  81.4 us

profile of v4, /device:TPU:1, one launch (start us, length us, event | category | flops | bytes accessed | tf_op | source)
XLA Modules:
  0.0 83.7 jit_solution(4236478278832558061)
XLA Ops:
  0.6 81.4 %shampoo.1 = (f32[32,64]{1,0:T(8,128)}, f32[256,128]{1,0:T(8,128)}, f32[32,256]{1,0:T(8,128)}) custom-call(bf16[1536,1024]{1,0:T(8,128)(2,1)} %act_hbm.1, bf16[1536,256]{1,0:T(8,128)(2,1)} %dy_hbm.1, f32[32,64]{1,0:T(8,128)} %bitcast.4, f32[256,128]{1,0:T(8,128)} %right_hbm.1, f32[8,128]{1,0:T(8,128)} %bitcast.6, f32[32,128]{1,0:T(8,128)} %bitcast.5), custom_call_target="tpu_custom_call" | custom-call | tf_op jit(solution)/shard_map/shampoo/pallas_call | solution.py:659
  82.1 1.6 %store.1 = (f32[32,64]{1,0:T(8,128)}, f32[256,128]{1,0:T(8,128)}, f32[32,256]{1,0:T(8,128)}) custom-call(f32[32,64]{1,0:T(8,128)} %get-tuple-element.9.left, f32[256,128]{1,0:T(8,128)} %get-tuple-element.10.right, f32[32,256]{1,0:T(8,128)} %get-tuple-element.11.update), custom_call_target="tpu_custom_call" | custom-call | tf_op jit(solution)/shard_map/store/pallas_call | solution.py:681

commit v5 on v4

--- a/solution.py
+++ b/solution.py
@@ -116,9 +116,9 @@
     lrow,
     lrows,
     terms,
-    xterm,
-    sums,
-    cterm,
+    tcore,
+    tx,
+    tcross,
     wrow,
     abuf,
     arecv,
@@ -148,6 +148,8 @@
     core_peer = (dp + 1 - 2 * c, mp, pre)
     x_peer = (dp + 2 - 4 * xl, mp, pre)
     hi_peer = (dp, 1 - mp, pre)
+    cross_peer = (dp + 3 - 4 * xl - 2 * c, mp, pre)
+    quad = (core_peer, x_peer, cross_peer)
 
     turn = (z - a // 2 + ny // 2 + nz) % nz
     goal_hi = jnp.where(xl == a % 2, mp, 1 - mp)
@@ -201,6 +203,7 @@
     greet(core_peer)
     greet(x_peer)
     greet(hi_peer)
+    greet(cross_peer)
     for o in range(1, nz):
         greet(z_peer(o))
     for o in range(1, ny):
@@ -287,25 +290,24 @@
     class Sum:
         def __init__(self, buf, recv, zrecv):
             self.buf, self.recv, self.zrecv = buf, recv, zrecv
-            self.ic, self.ix = net.slot(), net.slot()
+            self.iq = [net.slot() for _ in quad]
             self.iz = [net.slot() for _ in range(nz)]
 
-        def over_core(self):
-            net.send(self.ic, self.buf.at[0], self.recv.at[0], core_peer)
-
-        def over_x(self):
-            net.arrive(self.ic, self.recv.at[0], core_peer)
-            self.buf[1] = self.buf[0] + self.recv[0]
-            net.send(self.ix, self.buf.at[1], self.recv.at[1], x_peer)
+        def over_quad(self):
+            for i, peer in zip(self.iq, quad):
+                net.send(i, self.buf.at[0], self.recv.at[i - self.iq[0]], peer)
 
         def over_z(self):
-            net.arrive(self.ix, self.recv.at[1], x_peer)
-            self.buf[2] = self.buf[1] + self.recv[1]
+            value = self.buf[0]
+            for i, peer in zip(self.iq, quad):
+                net.arrive(i, self.recv.at[i - self.iq[0]], peer)
+                value = value + self.recv[i - self.iq[0]]
+            self.buf[1] = value
             for o in far_first(nz):
-                net.send(self.iz[o], self.buf.at[2], self.zrecv.at[o], z_peer(o))
+                net.send(self.iz[o], self.buf.at[1], self.zrecv.at[o], z_peer(o))
 
         def total(self):
-            value = self.buf[2]
+            value = self.buf[1]
             for o in near_first(nz):
                 net.arrive(self.iz[o], self.zrecv.at[o], z_peer(o))
                 value = value + self.zrecv[o]
@@ -360,7 +362,7 @@
 
     dy_load.wait()
     first_value = grad_block(0)
-    pl.semaphore_wait(barrier, 5 + (nz - 1) + (ny - 1))
+    pl.semaphore_wait(barrier, 6 + (nz - 1) + (ny - 1))
     blocks_and_x(first, lambda i: grad_block(i) if i else first_value)
 
     for copy in other_loads:
@@ -369,12 +371,11 @@
     p_row = jnp.broadcast_to(p_right[pl.ds(dp, 1), :], (8, 128))
     old_right = dot3(halves(p_row), halves(right_old[...]), NT)
     abuf[0] = jnp.where(row == 0, old_right[:, :HALF], old_right[:, HALF:])
-    old_sum.over_core()
+    old_sum.over_quad()
     for z_ in range(nz):
         prod[slab_rows(z_, 1 - xl), :] = jnp.zeros((SLAB, HALF), F32)
     for o in z_order[: nz // 2]:
         first.over_z(o)
-    old_sum.over_x()
     for o in z_order[nz // 2 :]:
         first.over_z(o)
     old_sum.over_z()
@@ -476,7 +477,7 @@
 
     blocks_and_x(second, prod_block)
     left_rows()
-    cut = [4, 5] if nz > 5 else [1, 1]
+    cut = [2, 4, 7] if nz > 6 else [1, 1, 1]
     for o in z_order[: cut[0]]:
         second.over_z(o)
     right_images()
@@ -487,9 +488,11 @@
     own_lanes = lrow.at[:, l_lanes(pre)]
     for o in far_first(ny):
         net.send(ilg[o], own_lanes, own_lanes, y_peer(o))
-    for o in z_order[cut[1] :]:
+    for o in z_order[cut[1] : cut[2]]:
         second.over_z(o)
     image_sum.over_y()
+    for o in z_order[cut[2] :]:
+        second.over_z(o)
 
     for o in near_first(ny):
         net.arrive(ilg[o], lrow.at[:, l_lanes(y_at(ny - o))], y_peer(ny - o))
@@ -511,33 +514,32 @@
         fbuf[0, pl.ds(j, 1), :] = left_image[:, j * 128 : (j + 1) * 128]
     left_square = jnp.sum(f_left * f_left, axis=0, keepdims=True)
     fbuf[0, pl.ds(rows_l, 8), :] = jnp.broadcast_to(left_square, (8, 128))
-    left_sum.over_core()
-
-    iz2 = [net.slot() for _ in range(nz)]
-    i_prod, i_term_x, i_term_c = net.slot(), net.slot(), net.slot()
-    prod[slab_rows(z, xl), :] = second.total()
-    own_prod = prod.at[slab_rows(z, xl), :]
-    for o in far_first(nz):
-        net.send(iz2[o], own_prod, own_prod, z_peer(o))
-
-    def rows_of(c_):
-        return pl.ds(pl.multiple_of((z * 2 + xl) * SLAB + c_ * 32, 32), 32)
-
-    net.send(i_prod, prod.at[rows_of(1 - c), :], wrow, core_peer)
-    left_sum.over_x()
+    left_sum.over_quad()
 
     whole = image_sum.total()
     norm_right = jnp.sqrt(whole[1:2, 0:1] + FLOOR)
     scaled = whole[0:1, :] / norm_right
     right_part = jnp.sum(scaled * scaled, axis=1, keepdims=True)
     cbuf[0] = jnp.broadcast_to(right_part, (8, 128))
-    last_sum.over_core()
+    last_sum.over_quad()
+
+    iz2 = [net.slot() for _ in range(nz)]
+    i_prod = net.slot()
+    i_term = [net.slot() for _ in quad]
+    prod[slab_rows(z, xl), :] = second.total()
+    own_prod = prod.at[slab_rows(z, xl), :]
+    for o in far_first(nz):
+        net.send(iz2[o], own_prod, own_prod, z_peer(o))
+
+    def rows_of(c_):
+        return pl.ds(pl.multiple_of((z * 2 + xl) * SLAB + c_ * 32, 32), 32)
+
+    net.send(i_prod, prod.at[rows_of(1 - c), :], wrow, core_peer)
 
     left_grad = dot3(halves(lrow[...]), grad_split, NN)
     right_out[...] = rtile[...].T
     lanes = lrow[:, old_lanes]
     left_out[...] = jnp.where(a % 2 == 0, lanes[:, :SLAB], lanes[:, SLAB:])
-    last_sum.over_x()
     left_sum.over_z()
     last_sum.over_z()
     net.arrive(i_rows_x, l_rows(1 - xl, c), x_peer)
@@ -555,10 +557,12 @@
         )
     terms[...] = term
 
-    def term_rows(xl_):
-        return pl.ds(pl.multiple_of(xl_ * SLAB, SLAB), SLAB)
-
-    net.send(i_term_x, terms.at[term_rows(1 - xl), :], xterm, x_peer)
+    def term_rows(xl_, c_):
+        return pl.ds(pl.multiple_of((xl_ * 2 + c_) * 32, 32), 32)
+
+    net.send(i_term[1], terms.at[term_rows(1 - xl, c), :], tx, x_peer)
+    net.send(i_term[2], terms.at[term_rows(1 - xl, 1 - c), :], tcross, cross_peer)
+    net.send(i_term[0], terms.at[term_rows(xl, 1 - c), :], tcore, core_peer)
     top_right = jnp.sqrt(last_sum.total()[0:1, 0:1] + FLOOR)
     images = left_sum.total()
     norm_left = jnp.sqrt(images[rows_l : rows_l + 1, 0:1] + FLOOR)
@@ -569,19 +573,14 @@
     )
     scale = lax.rsqrt(jnp.sqrt(top_left * top_right)) * 0.0625
     rest = 5.0 * (5.0 * grad[own32, :] - left_grad / top_left)
-    net.arrive(i_term_x, xterm, x_peer)
-    sums[...] = terms[term_rows(xl), :] + xterm[...]
-
-    def sum_rows(c_):
-        return pl.ds(pl.multiple_of(c_ * 32, 32), 32)
-
-    net.send(i_term_c, sums.at[sum_rows(1 - c), :], cterm, core_peer)
     update_out[...] = rest
-    by_right = (sums[sum_rows(c), :] / top_left - 5.0 * prod[rows_of(c), :]) / top_right
+    net.arrive(i_prod, wrow, core_peer)
+    net.arrive(i_term[0], tcore, core_peer)
+    net.arrive(i_term[1], tx, x_peer)
+    by_right = ((terms[term_rows(xl, c), :] + tx[...]) / top_left - 5.0 * prod[rows_of(c), :]) / top_right
     update_out[:, mine] = (update_out[:, mine] + by_right) * scale
-    net.arrive(i_prod, wrow, core_peer)
-    net.arrive(i_term_c, cterm, core_peer)
-    by_right = (cterm[...] / top_left - 5.0 * wrow[...]) / top_right
+    net.arrive(i_term[2], tcross, cross_peer)
+    by_right = ((tcore[...] + tcross[...]) / top_left - 5.0 * wrow[...]) / top_right
     update_out[:, other] = (update_out[:, other] + by_right) * scale
 
     net.finish()
@@ -632,24 +631,24 @@
         vmem((32, d_model), F32),
         vmem((128, d_model), F32),
         vmem((128, HALF), F32),
-        vmem((SLAB, HALF), F32),
-        vmem((SLAB, HALF), F32),
         vmem((32, HALF), F32),
         vmem((32, HALF), F32),
+        vmem((32, HALF), F32),
+        vmem((32, HALF), F32),
+        vmem((2, 8, 128), F32),
         vmem((3, 8, 128), F32),
-        vmem((2, 8, 128), F32),
         vmem((nz, 8, 128), F32),
         vmem((2, rows_l, 128), F32),
         vmem((rows_l, 128), F32),
         vmem((ny, rows_l, 128), F32),
+        vmem((2, rows_l + 8, 128), F32),
         vmem((3, rows_l + 8, 128), F32),
-        vmem((2, rows_l + 8, 128), F32),
         vmem((nz, rows_l + 8, 128), F32),
         vmem((2, 8, 128), F32),
         vmem((8, 128), F32),
         vmem((ny, 8, 128), F32),
+        vmem((2, 8, 128), F32),
         vmem((3, 8, 128), F32),
-        vmem((2, 8, 128), F32),
         vmem((nz, 8, 128), F32),
         pltpu.SemaphoreType.DMA((COPIES,)),
         pltpu.SemaphoreType.DMA((COPIES,)),

time: 83.8 us -> 84.1 us (level)
  no operation moved by 1% of the time
where the time goes in v5:
time: 84.1 us; the launch traced here: 83.9 us
  Pallas kernels  83.3 us (99%)
    pallas_call x1, Pallas kernels, step(): pl.pallas_call(functools.partial(kernel, nz, ny, ff), out_shape=(jax.Shap...  81.7 us

profile of v5, /device:TPU:1, one launch (start us, length us, event | category | flops | bytes accessed | tf_op | source)
XLA Modules:
  0.0 83.9 jit_solution(9931427409451632314)
XLA Ops:
  0.6 81.7 %shampoo.1 = (f32[32,64]{1,0:T(8,128)}, f32[256,128]{1,0:T(8,128)}, f32[32,256]{1,0:T(8,128)}) custom-call(bf16[1536,1024]{1,0:T(8,128)(2,1)} %act_hbm.1, bf16[1536,256]{1,0:T(8,128)(2,1)} %dy_hbm.1, f32[32,64]{1,0:T(8,128)} %bitcast.4, f32[256,128]{1,0:T(8,128)} %right_hbm.1, f32[8,128]{1,0:T(8,128)} %bitcast.6, f32[32,128]{1,0:T(8,128)} %bitcast.5), custom_call_target="tpu_custom_call" | custom-call | tf_op jit(solution)/shard_map/shampoo/pallas_call | solution.py:658
  82.3 1.6 %store.1 = (f32[32,64]{1,0:T(8,128)}, f32[256,128]{1,0:T(8,128)}, f32[32,256]{1,0:T(8,128)}) custom-call(f32[32,64]{1,0:T(8,128)} %get-tuple-element.9.left, f32[256,128]{1,0:T(8,128)} %get-tuple-element.10.right, f32[32,256]{1,0:T(8,128)} %get-tuple-element.11.update), custom_call_target="tpu_custom_call" | custom-call | tf_op jit(solution)/shard_map/store/pallas_call | solution.py:680

commit v6 on v5

--- a/solution.py
+++ b/solution.py
@@ -477,7 +477,7 @@
 
     blocks_and_x(second, prod_block)
     left_rows()
-    cut = [2, 4, 7] if nz > 6 else [1, 1, 1]
+    cut = [5, 6, 8] if nz > 7 else [1, 1, 1]
     for o in z_order[: cut[0]]:
         second.over_z(o)
     right_images()
@@ -494,6 +494,20 @@
     for o in z_order[cut[2] :]:
         second.over_z(o)
 
+
+    iz2 = [net.slot() for _ in range(nz)]
+    i_prod = net.slot()
+    i_term = [net.slot() for _ in quad]
+    prod[slab_rows(z, xl), :] = second.total()
+    own_prod = prod.at[slab_rows(z, xl), :]
+    for o in far_first(nz):
+        net.send(iz2[o], own_prod, own_prod, z_peer(o))
+
+    def rows_of(c_):
+        return pl.ds(pl.multiple_of((z * 2 + xl) * SLAB + c_ * 32, 32), 32)
+
+    net.send(i_prod, prod.at[rows_of(1 - c), :], wrow, core_peer)
+
     for o in near_first(ny):
         net.arrive(ilg[o], lrow.at[:, l_lanes(y_at(ny - o))], y_peer(ny - o))
 
@@ -522,19 +536,6 @@
     right_part = jnp.sum(scaled * scaled, axis=1, keepdims=True)
     cbuf[0] = jnp.broadcast_to(right_part, (8, 128))
     last_sum.over_quad()
-
-    iz2 = [net.slot() for _ in range(nz)]
-    i_prod = net.slot()
-    i_term = [net.slot() for _ in quad]
-    prod[slab_rows(z, xl), :] = second.total()
-    own_prod = prod.at[slab_rows(z, xl), :]
-    for o in far_first(nz):
-        net.send(iz2[o], own_prod, own_prod, z_peer(o))
-
-    def rows_of(c_):
-        return pl.ds(pl.multiple_of((z * 2 + xl) * SLAB + c_ * 32, 32), 32)
-
-    net.send(i_prod, prod.at[rows_of(1 - c), :], wrow, core_peer)
 
     left_grad = dot3(halves(lrow[...]), grad_split, NN)
     right_out[...] = rtile[...].T

time: 84.1 us -> 82.2 us (0.977)
  Pallas kernels: 83.3 us -> 81.4 us
    pallas_call x1, Pallas kernels: 81.7 us -> 79.8 us  [step(): pl.pallas_call(functools.partial(kernel, nz, ny, ff), out_shape=(jax.Shap...]
where the time goes in v6:
time: 82.2 us; the launch traced here: 82.1 us
  Pallas kernels  81.4 us (99%)
    pallas_call x1, Pallas kernels, step(): pl.pallas_call(functools.partial(kernel, nz, ny, ff), out_shape=(jax.Shap...  79.8 us

profile of v6, /device:TPU:1, one launch (start us, length us, event | category | flops | bytes accessed | tf_op | source)
XLA Modules:
  0.0 82.1 jit_solution(7106572125494970753)
XLA Ops:
  0.6 79.8 %shampoo.1 = (f32[32,64]{1,0:T(8,128)}, f32[256,128]{1,0:T(8,128)}, f32[32,256]{1,0:T(8,128)}) custom-call(bf16[1536,1024]{1,0:T(8,128)(2,1)} %act_hbm.1, bf16[1536,256]{1,0:T(8,128)(2,1)} %dy_hbm.1, f32[32,64]{1,0:T(8,128)} %bitcast.4, f32[256,128]{1,0:T(8,128)} %right_hbm.1, f32[8,128]{1,0:T(8,128)} %bitcast.6, f32[32,128]{1,0:T(8,128)} %bitcast.5), custom_call_target="tpu_custom_call" | custom-call | tf_op jit(solution)/shard_map/shampoo/pallas_call | solution.py:659
  80.5 1.6 %store.1 = (f32[32,64]{1,0:T(8,128)}, f32[256,128]{1,0:T(8,128)}, f32[32,256]{1,0:T(8,128)}) custom-call(f32[32,64]{1,0:T(8,128)} %get-tuple-element.9.left, f32[256,128]{1,0:T(8,128)} %get-tuple-element.10.right, f32[32,256]{1,0:T(8,128)} %get-tuple-element.11.update), custom_call_target="tpu_custom_call" | custom-call | tf_op jit(solution)/shard_map/store/pallas_call | solution.py:681
